TPU v7x, 32 devices: a whole 2x2x4 slice. The times are simulated.
32 devices in a mesh: pb: 4 (over z), pa: 8 (over y, x, core).
Axes of the slice: x: 2, y: 2, z: 4, core: 2. Of those that a mesh axis runs over, the one named last changes fastest.
Arguments:
- queries: bfloat16 [4096, 3584], P(('pb', 'pa')), may hold values from -16 to 16
- passages: bfloat16 [16384, 3584], P(('pb', 'pa')), may hold values from -16 to 16
- hard_block_offsets: int32 [1024, 4], P(('pb', 'pa')), may hold values from 0 to 30, all different within a row; in each aligned block of 32 rows (0 to 31, 32 to 63, ...) at most 8 rows name the same one
- positive: int32 [4096], P(('pb', 'pa')), may hold values from 0 to 511
- context: bfloat16 [16384, 3584], P(('pb', 'pa')), may hold values from -6 to 6
- residual: bfloat16 [16384, 3584], P(('pb', 'pa')), may hold values from -6 to 6
- output_weight: bfloat16 [3584, 3584], P(('pb', 'pa')), may hold values from -0.09375 to 0.09375
- adapter_down_weight: bfloat16 [3584, 16], replicated, may hold values from -0.09375 to 0.09375
- adapter_up_weight: bfloat16 [16, 3584], replicated, may hold values from -1.5 to 1.5
- final_norm_weight: bfloat16 [3584], replicated, may hold values from 0.099609375 to 1.8984375
Outputs:
- query_gradient: float32 [4096, 3584], P(('pb', 'pa'))
- grad_passages: float32 [16384, 3584], P(('pb', 'pa'))
- grad_lora_down: float32 [3584, 16], P(('pb', 'pa'))
- grad_lora_up: float32 [16, 3584], P(None, ('pb', 'pa'))
Inputs may be any that keep to these rules, and one draw needn't show every extreme that they name: `hard_block_offsets`: each row lists 4 different offsets. Query block k is paired with passage block (k // 32 + 1 + offset) modulo the number of devices. In each aligned block of 32 rows no offset appears more than 8 times, and some offset appears exactly 8 times.
All inputs are finite; a program needn't handle non-finite values.
Results may differ from a plain program's by a relative error of at most 0.0045.
Values may be sent and summed in bfloat16 or wider, within the bound.
No kernel may reach another device: no remote copies, remote signals or barrier semaphores. Data moves between devices by JAX's collectives and lax.ppermute only.
A program may use at most 192 MiB of HBM per device.

v0:
```python
import math

import jax
import jax.numpy as jnp
from jax import lax
from jax.sharding import PartitionSpec as P

MODEL_WIDTH = 3584
RERUN_QUERIES = 16
TQ = 32


inverse_temp = 2.0
loss_scale = 32.0
adapter_scale = 2.0
epsilon = 1e-06
absent_mass = 1e30


def slot_layout(offsets, source, device_count, capacity):
    flat_offsets = offsets.reshape(-1)
    target = (source + 1 + flat_offsets) % device_count
    pair_order = jnp.arange(flat_offsets.shape[0], dtype=jnp.int32)
    earlier = (target[:, None] == target[None, :]) & (pair_order[:, None] > pair_order[None, :])
    slot_rank = jnp.sum(earlier.astype(jnp.int32), axis=1)
    slot_index = target * capacity + slot_rank
    slot_block = (
        jnp.full((device_count * capacity,), -1, jnp.int32)
        .at[slot_index]
        .set(pair_order // offsets.shape[1])
    )
    return (slot_index, slot_block)


def partial_softmax(query_rows, passage_rows, score_scale):
    scores = jnp.dot(query_rows, passage_rows.T, preferred_element_type=jnp.float32) * score_scale
    row_peak = jnp.max(scores, axis=1)
    weights = jnp.exp(scores - row_peak[:, None])
    row_mass = jnp.sum(weights, axis=1)
    row_mean = (
        jnp.dot(weights.astype(jnp.bfloat16), passage_rows, preferred_element_type=jnp.float32)
        / row_mass[:, None]
    )
    return (scores, row_peak + jnp.log(row_mass), row_mean)


def merge_partials(near_mass, near_mean, far_mass, far_mean):
    block_count, hard_count, block_rows = far_mass.shape
    far_rows = jnp.transpose(far_mass, (0, 2, 1)).reshape(block_count * block_rows, hard_count)
    every_mass = jnp.concatenate([near_mass[:, None], far_rows], axis=1)
    mass_peak = jnp.max(every_mass, axis=1)
    log_total = mass_peak + jnp.log(jnp.sum(jnp.exp(every_mass - mass_peak[:, None]), axis=1))
    near_share = jnp.exp(near_mass - log_total)
    far_share = jnp.exp(far_mass - log_total.reshape(block_count, 1, block_rows))
    far_part = jnp.sum(far_mean * far_share[..., None], axis=1).reshape(
        block_count * block_rows, -1
    )
    return (log_total, near_share[:, None] * near_mean + far_part)


def layer_parts(
    context,
    residual,
    frozen_output,
    adapter_down_weight,
    adapter_up_weight,
    final_norm_weight,
    output_gradient,
):
    token_count = context.shape[0]
    narrow_projection = jnp.dot(
        context, adapter_down_weight, preferred_element_type=jnp.float32
    ).astype(jnp.bfloat16)
    hidden_state = (
        residual.astype(jnp.float32)
        + frozen_output
        + adapter_scale
        * jnp.dot(narrow_projection, adapter_up_weight, preferred_element_type=jnp.float32)
    )
    inverse_rms = lax.rsqrt(jnp.mean(hidden_state * hidden_state, axis=1, keepdims=True) + epsilon)
    spread_cot = jnp.broadcast_to(
        output_gradient[:, None, :] / TQ, (output_gradient.shape[0], TQ, output_gradient.shape[1])
    ).reshape(token_count, -1)
    scaled = final_norm_weight.astype(jnp.float32)[None, :] * spread_cot
    grad_hidden = inverse_rms * scaled - hidden_state * inverse_rms**3 * jnp.mean(
        hidden_state * scaled, axis=1, keepdims=True
    )
    gradient_lowered = grad_hidden.astype(jnp.bfloat16)
    product_dims = (((0,), (0,)), ((), ()))
    up_product = (
        adapter_scale
        * lax.dot_general(
            narrow_projection, gradient_lowered, product_dims, preferred_element_type=jnp.float32
        )
        / RERUN_QUERIES
    )
    gradient_narrow = (
        adapter_scale
        * jnp.dot(gradient_lowered, adapter_up_weight.T, preferred_element_type=jnp.float32)
    ).astype(jnp.bfloat16)
    down_term = (
        lax.dot_general(context, gradient_narrow, product_dims, preferred_element_type=jnp.float32)
        / RERUN_QUERIES
    )
    return (down_term, up_product)


def local(
    queries,
    passages,
    hard_block_offsets,
    positive,
    context,
    residual,
    output_weight,
    adapter_down_weight,
    adapter_up_weight,
    final_norm_weight,
):
    device_count = lax.axis_size(("pb", "pa"))
    block_count, hard_count = hard_block_offsets.shape
    block_rows = queries.shape[0] // block_count
    capacity = 2 * block_count * hard_count // device_count
    slot_width = capacity * block_rows
    passage_count = passages.shape[0]
    score_scale = inverse_temp / math.sqrt(MODEL_WIDTH)
    whole_weight = lax.all_gather(output_weight, ("pb", "pa"), axis=0, tiled=True)
    frozen_output = jnp.dot(context, whole_weight, preferred_element_type=jnp.float32)
    own_index = lax.axis_index(("pb", "pa"))
    slot_index, slot_block = slot_layout(hard_block_offsets, own_index, device_count, capacity)
    slot_filled = slot_block >= 0
    query_blocks = queries.reshape(block_count, block_rows, MODEL_WIDTH)
    outgoing = jnp.where(
        slot_filled[:, None, None],
        query_blocks[jnp.maximum(slot_block, 0)],
        jnp.zeros((), queries.dtype),
    )
    outgoing = outgoing.reshape(device_count, slot_width, MODEL_WIDTH)
    arrived = lax.all_to_all(outgoing, ("pb", "pa"), split_axis=0, concat_axis=0, tiled=True)
    arrived = arrived.reshape(-1, MODEL_WIDTH)
    near_scores, near_mass, near_mean = partial_softmax(queries, passages, score_scale)
    far_scores, far_mass, far_mean = partial_softmax(arrived, passages, score_scale)
    far_mean = far_mean.astype(jnp.bfloat16)
    returned_mean = lax.all_to_all(
        far_mean.reshape(device_count, slot_width, MODEL_WIDTH),
        ("pb", "pa"),
        split_axis=0,
        concat_axis=0,
        tiled=True,
    )
    returned_mass = lax.all_to_all(
        far_mass.reshape(device_count, slot_width),
        ("pb", "pa"),
        split_axis=0,
        concat_axis=0,
        tiled=True,
    )
    returned_mean = returned_mean.reshape(device_count * capacity, block_rows, MODEL_WIDTH)[
        slot_index
    ]
    returned_mass = returned_mass.reshape(device_count * capacity, block_rows)[slot_index]
    returned_mean = returned_mean.reshape(block_count, hard_count, block_rows, MODEL_WIDTH)
    returned_mass = returned_mass.reshape(block_count, hard_count, block_rows)
    log_total, mixed = merge_partials(near_mass, near_mean, returned_mass, returned_mean)
    positive_hot = positive[:, None] == jnp.arange(passage_count, dtype=jnp.int32)[None, :]
    positive_rows = jnp.dot(
        positive_hot.astype(jnp.bfloat16), passages, preferred_element_type=jnp.float32
    )
    query_gradient = loss_scale * score_scale * (mixed - positive_rows)
    log_blocks = log_total.reshape(block_count, block_rows)
    log_outgoing = jnp.where(
        slot_filled[:, None], log_blocks[jnp.maximum(slot_block, 0)], absent_mass
    )
    log_arrived = lax.all_to_all(
        log_outgoing.reshape(device_count, slot_width),
        ("pb", "pa"),
        split_axis=0,
        concat_axis=0,
        tiled=True,
    ).reshape(-1)
    far_weight = jnp.exp(far_scores - log_arrived[:, None]).astype(jnp.bfloat16)
    near_weight = (
        jnp.exp(near_scores - log_total[:, None]) - positive_hot.astype(jnp.float32)
    ).astype(jnp.bfloat16)
    product_dims = (((0,), (0,)), ((), ()))
    far_grad = lax.dot_general(
        far_weight, arrived, product_dims, preferred_element_type=jnp.float32
    )
    near_grad = lax.dot_general(
        near_weight, queries, product_dims, preferred_element_type=jnp.float32
    )
    grad_passages = loss_scale * score_scale * (far_grad + near_grad)
    down_term, up_product = layer_parts(
        context,
        residual,
        frozen_output,
        adapter_down_weight,
        adapter_up_weight,
        final_norm_weight,
        query_gradient[:RERUN_QUERIES],
    )
    grad_down, grad_up = (
        lax.psum_scatter(down_term, ("pb", "pa"), scatter_dimension=0, tiled=True),
        lax.psum_scatter(up_product, ("pb", "pa"), scatter_dimension=1, tiled=True),
    )
    return (query_gradient, grad_passages, grad_down, grad_up)


def solution(mesh):
    placed = (
        P(("pb", "pa"), None),
        P(("pb", "pa"), None),
        P(("pb", "pa"), None),
        P(("pb", "pa")),
        P(("pb", "pa"), None),
        P(("pb", "pa"), None),
        P(("pb", "pa"), None),
        P(),
        P(),
        P(),
    )
    return jax.shard_map(
        local,
        mesh=mesh,
        in_specs=placed,
        out_specs=(
            P(("pb", "pa"), None),
            P(("pb", "pa"), None),
            P(("pb", "pa"), None),
            P(None, ("pb", "pa")),
        ),
        check_vma=False,
    )
```

profile of v0, /device:TPU:0, one launch (start us, length us, event | category | flops | bytes accessed | tf_op | source)
XLA Modules:
  0.0 860.6 jit_solution(14025059238002213129)
XLA Ops:
  7.2 0.7 all-gather.2.cloned.1.call-update
  7.9 0.7 broadcast_add_fusion
  8.6 0.1 copy.37
  8.7 0.1 add.179
  8.8 0.1 add.177
  8.9 0.2 convert_reduce_fusion
  9.1 1.0 scatter_custom_fusion
  10.1 0.1 broadcast_in_dim.33
  10.2 0.1 copy.39
  10.3 0.1 copy.40
  10.4 1.8 reshape.300
  12.3 13.1 %gather_fusion = bf16[256,4,3584]{2,1,0:T(4,128)(2,1)} fusion(bf16[32,4,3584]{2,1,0:T(4,128)(2,1)S(1)} %reshape.300, s32[1024]{0:T(1024)S(1)} %pad_clamp_fusion.1), kind=kCustom, calls=%fused_computation | custom fusion | bytes 14681088 | tf_op jit(solution)/shard_map/gather | solution.py:135
  25.4 12.1 %gather.17 = bf16[32,32,3584]{2,1,0:T(8,128)(2,1)} reshape(bf16[256,4,3584]{2,1,0:T(4,128)(2,1)} %gather_fusion) | data formatting | bytes 14680064 | tf_op jit(solution)/shard_map/gather | solution.py:135
  37.5 6.7 broadcast_select_fusion
  44.2 7.4 all-to-all-start
  51.6 3.4 fusion.42
  55.1 0.2 fusion.20
  55.3 257.0 %all-to-all-done = bf16[32,32,3584]{2,1,0:T(8,128)(2,1)} async-done(((bf16[32,32,3584]{2,1,0:T(8,128)(2,1)}), bf16[32,32,3584]{2,1,0:T(8,128)(2,1)}, u32[]{:S(2)}, u32[]{:S(2)}) %all-to-all-start) | async-done | bytes 7340064 | tf_op jit(solution)/shard_map/all_to_all | solution.py:139
  312.3 7.4 multiply_reduce_fusion.1
  319.7 1.3 copy-done.6
  321.0 0.4 fusion.11
  321.4 0.7 add.184
  322.1 3.6 all-to-all-start.1
  325.7 7.1 all-to-all-done.1
  332.8 0.5 broadcast.226
  333.3 0.7 reduce.9
  334.0 0.1 reshape.302
  334.1 0.6 gather_fusion.1
  334.8 0.1 reduce_max.52
  334.9 0.1 add.187
  335.0 0.1 reshape.304
  335.2 0.1 log.61
  335.3 0.7 gather_fusion.3
  336.0 0.1 gather.21
  336.1 0.1 copy.42
  336.2 0.7 copy.43
  336.9 2.7 all-to-all-start.3
  339.6 9.8 %divide_convert_fusion = bf16[1024,3584]{1,0:T(8,128)(2,1)} fusion(f32[1024]{0:T(1024)S(1)} %fusion.11, bf16[512,3584]{1,0:T(8,128)(2,1)} %param.11, f32[1024,512]{0,1:T(8,128)} %copy-done.6, f32[1024]{0:T(1024)S(1)} %get-tuple-element.13), kind=kOutput, calls=%fused_computation.5 | convolution fusion | flops 3767009280 | bytes 13115392 | tf_op jit(solution)/shard_map/dot_general | solution.py:41
  349.4 6.1 all-to-all-start.2
  355.6 3.1 convolution_convert_fusion
  358.7 0.7 reduce.10
  359.4 0.1 sub.87
  359.5 10.6 %fusion.14 = f32[512,3584]{1,0:T(8,128)} fusion(bf16[1024,3584]{1,0:T(8,128)(2,1)} %bitcast.3, f32[1024,512]{0,1:T(8,128)} %copy-done.6, f32[1024]{0:T(1024)S(1)} %sub.87), kind=kOutput, calls=%fused_computation.35 | convolution fusion | flops 3759669248 | bytes 16781312 | tf_op jit(solution)/shard_map/dot_general | solution.py:186
  370.1 148.3 %all-to-all-done.2 = bf16[32,32,3584]{2,1,0:T(8,128)(2,1)} async-done(((bf16[32,32,3584]{2,1,0:T(8,128)(2,1)}), bf16[32,32,3584]{2,1,0:T(8,128)(2,1)}, u32[]{:S(2)}, u32[]{:S(2)}) %all-to-all-start.2) | async-done | bytes 7340064 | tf_op jit(solution)/shard_map/all_to_all | solution.py:144
  518.5 12.8 %reshape.306 = bf16[256,4,3584]{2,1,0:T(4,128)(2,1)} reshape(bf16[32,32,3584]{2,1,0:T(8,128)(2,1)} %all-to-all-done.2) | data formatting | bytes 14680064 | tf_op jit(solution)/shard_map/reshape | solution.py:158
  531.3 8.4 gather_fusion.2
  539.7 5.2 fusion
  544.8 1.9 reshape.307
  546.7 3.5 fusion.8
  550.2 0.2 copy-done.2
  550.4 0.7 fusion.6
  551.2 20.3 %fusion.43 = f32[512,3584]{1,0:T(8,128)S(1)} fusion(bf16[512,3584]{1,0:T(8,128)(2,1)} %param.14, bf16[3584,3584]{1,0:T(8,128)(2,1)} %all-gather.2.cloned.1.call-done), kind=kOutput, calls=%fused_computation.97 | convolution fusion | flops 13153337344 | bytes 36700160 | tf_op jit(solution)/shard_map/dot_general | solution.py:128
  571.6 2.6 multiply_reduce_fusion
  574.1 2.5 fusion.4
  576.7 1.8 copy-done.1
  578.5 0.6 convolution_multiply_fusion
  579.1 1.8 copy.46
  581.0 4.8 fusion.9
  585.8 1.8 copy.44
  587.6 7.4 add_multiply_fusion
  595.0 121.6 %reduce-scatter.9.cloned.1.call-done = f32[112,16]{1,0:T(8,128)} async-done(((f32[3584,16]{1,0:T(8,128)}), f32[112,16]{1,0:T(8,128)}) %reduce-scatter.9.cloned.1.call-update) | async-done | bytes 7184
  716.5 1.5 copy.47
  718.0 134.2 %reduce-scatter.7.cloned.1.call-done = f32[112,16]{1,0:T(8,128)} async-done(((f32[3584,16]{1,0:T(8,128)}), f32[112,16]{1,0:T(8,128)}) %reduce-scatter.7.cloned.1.call-update) | async-done | bytes 7184
  852.2 1.5 copy.45
  (44 shorter events, 0.4 us)
Async XLA Ops:
  7.2 564.4 %copy-start = (bf16[16,3584]{1,0:T(8,128)(2,1)S(1)}, bf16[16,3584]{1,0:T(8,128)(2,1)}, u32[]{:S(2)}) copy-start(bf16[16,3584]{1,0:T(8,128)(2,1)} %param.18) | copy-start | bytes 344068
  7.2 544.0 %all-gather.2.cloned.1.call-start = ((), (), s32[]{:S(2)}) async-start(), calls=%async_computation.6 | async-start | bytes 26492928 | tf_op jit(solution)/shard_map/all_gather | solution.py:127
  44.2 7.4 copy-start.3
  44.2 268.1 %all-to-all-start = ((bf16[32,32,3584]{2,1,0:T(8,128)(2,1)}), bf16[32,32,3584]{2,1,0:T(8,128)(2,1)}, u32[]{:S(2)}, u32[]{:S(2)}) async-start(bf16[32,32,3584]{2,1,0:T(8,128)(2,1)} %broadcast_select_fusion), calls=%async_computation | async-start | bytes 14680064 | tf_op jit(solution)/shard_map/all_to_all | solution.py:139
  319.7 1.3 copy-start.6
  322.1 10.7 %all-to-all-start.1 = ((f32[32,1,32]{2,1,0:T(1,128)}), f32[32,1,32]{2,1,0:T(1,128)S(1)}, u32[]{:S(2)}, u32[]{:S(2)}) async-start(f32[32,1,32]{2,1,0:T(1,128)} %add.184), calls=%async_computation.1 | async-start | bytes 32768 | tf_op jit(solution)/shard_map/all_to_all | solution.py:151
  336.9 12.5 %all-to-all-start.3 = ((f32[32,1,32]{2,1,0:T(1,128)}), f32[32,1,32]{2,1,0:T(1,128)S(1)}, u32[]{:S(2)}, u32[]{:S(2)}) async-start(f32[32,1,32]{2,1,0:T(1,128)} %copy.43), calls=%async_computation.3 | async-start | bytes 32768 | tf_op jit(solution)/shard_map/all_to_all | solution.py:174
  349.4 6.1 copy-start.8
  349.4 6.1 copy-start.7
  349.4 169.0 %all-to-all-start.2 = ((bf16[32,32,3584]{2,1,0:T(8,128)(2,1)}), bf16[32,32,3584]{2,1,0:T(8,128)(2,1)}, u32[]{:S(2)}, u32[]{:S(2)}) async-start(bf16[32,32,3584]{2,1,0:T(8,128)(2,1)} %bitcast.62), calls=%async_computation.2 | async-start | bytes 14680064 | tf_op jit(solution)/shard_map/all_to_all | solution.py:144
  355.5 361.0 %reduce-scatter.9.cloned.1.call-start = ((), (), s32[]{:S(2)}) async-start(), calls=%async_computation.8 | async-start | bytes 1892352
  546.7 3.7 copy-start.2
  546.7 3.7 copy-start.9
  551.1 20.4 %copy-start.5 = (f32[128,3584]{1,0:T(8,128)}, f32[128,3584]{1,0:T(8,128)S(1)}, u32[]{:S(2)}) copy-start(f32[128,3584]{1,0:T(8,128)S(1)} %fusion.6) | copy-start | bytes 5505028
  551.2 20.3 %copy-start.4 = (bf16[512,3584]{1,0:T(8,128)(2,1)S(1)}, bf16[512,3584]{1,0:T(8,128)(2,1)}, u32[]{:S(2)}) copy-start(bf16[512,3584]{1,0:T(8,128)(2,1)} %param.15) | copy-start | bytes 11010052
  576.7 1.8 copy-start.1
  580.9 271.3 %reduce-scatter.7.cloned.1.call-start = ((), (), s32[]{:S(2)}) async-start(), calls=%async_computation.7 | async-start | bytes 1892352
Sparse Core Ops, SparseCore 0:
  10.8 289.8 all-gather.1
  581.1 135.4 reduce-scatter.8
  718.8 133.3 reduce-scatter.6
where the time goes:
time: 870 us; the launch traced here: 861 us
  waiting for transfers between devices  669 us (77%)
  matrix products  74.1 us (9%)
  local copies, waits for them, and re-layouts  65.6 us (8%)
  starting transfers between devices  19.9 us (2%)
  other arithmetic  17.5 us (2%)
  between operations  14.6 us (2%)
    all_to_all x1, waiting for transfers between devices, local(): lax.all_to_all(outgoing, ('pb', 'pa'), split_axis=0, concat_axis=0, tiled...  257 us
    unnamed x5, waiting for transfers between devices  256 us
    all_to_all x1, waiting for transfers between devices, local(): lax.all_to_all(far_mean.reshape(device_count, slot_width, MODEL_WIDTH), (...  148 us
    gather x2, local copies, waits for them, and re-layouts, local(): query_blocks[jnp.maximum(slot_block, 0)]  25.2 us
    dot_general x1, matrix products, local(): jnp.dot(context, whole_weight, preferred_element_type=jnp.float32)  20.3 us
  transfers between devices with their start and end apart: 7, of which 5 were waited for; matrix products, arithmetic and copies ran while one was open for 14% of the time, Pallas kernels for 0%

commit v1 on v0

v1 whole, which is shorter than its diff:
```python
import math

import jax
import jax.numpy as jnp
from jax import lax
from jax.sharding import PartitionSpec as P


MODEL_WIDTH = 3584
RERUN_QUERIES = 16
TQ = 32


inverse_temp = 2.0
loss_scale = 32.0
adapter_scale = 2.0
epsilon = 1e-06
absent_mass = 1e30


def slot_positions(offsets, source, device_count, capacity, block_rows):
    block_count, hard_count = offsets.shape
    flat_offsets = offsets.reshape(-1)
    target = (source + 1 + flat_offsets) % device_count
    pair_order = jnp.arange(flat_offsets.shape[0], dtype=jnp.int32)
    earlier = (target[:, None] == target[None, :]) & (pair_order[:, None] > pair_order[None, :])
    slot_rank = jnp.sum(earlier.astype(jnp.int32), axis=1)
    slot_index = (target * capacity + slot_rank).reshape(block_count, 1, hard_count)
    row = jnp.arange(block_rows, dtype=jnp.int32)[None, :, None]
    return (slot_index * block_rows + row).reshape(block_count * block_rows, hard_count)


def partial_softmax(query_rows, passage_rows, score_scale):
    scores = jnp.dot(query_rows, passage_rows.T, preferred_element_type=jnp.float32) * score_scale
    row_peak = jnp.max(scores, axis=1)
    weights = jnp.exp(scores - row_peak[:, None])
    row_mass = jnp.sum(weights, axis=1)
    row_mean = (
        jnp.dot(weights.astype(jnp.bfloat16), passage_rows, preferred_element_type=jnp.float32)
        / row_mass[:, None]
    )
    return (scores, row_peak + jnp.log(row_mass), row_mean)


def exchange(values):
    return lax.all_to_all(values, ("pb", "pa"), split_axis=0, concat_axis=0, tiled=True)


def layer_hidden(context, residual, whole_weight, adapter_down_weight, adapter_up_weight):
    narrow_projection = jnp.dot(
        context, adapter_down_weight, preferred_element_type=jnp.float32
    ).astype(jnp.bfloat16)
    frozen_output = jnp.dot(context, whole_weight, preferred_element_type=jnp.float32)
    hidden_state = (
        residual.astype(jnp.float32)
        + frozen_output
        + adapter_scale
        * jnp.dot(narrow_projection, adapter_up_weight, preferred_element_type=jnp.float32)
    )
    return (narrow_projection, hidden_state)


def layer_parts(
    context,
    narrow_projection,
    hidden_state,
    adapter_up_weight,
    final_norm_weight,
    output_gradient,
):
    token_count = context.shape[0]
    inverse_rms = lax.rsqrt(jnp.mean(hidden_state * hidden_state, axis=1, keepdims=True) + epsilon)
    spread_cot = jnp.broadcast_to(
        output_gradient[:, None, :] / TQ, (output_gradient.shape[0], TQ, output_gradient.shape[1])
    ).reshape(token_count, -1)
    scaled = final_norm_weight.astype(jnp.float32)[None, :] * spread_cot
    grad_hidden = inverse_rms * scaled - hidden_state * inverse_rms**3 * jnp.mean(
        hidden_state * scaled, axis=1, keepdims=True
    )
    gradient_lowered = grad_hidden.astype(jnp.bfloat16)
    product_dims = (((0,), (0,)), ((), ()))
    up_product = lax.dot_general(
        narrow_projection, gradient_lowered, product_dims, preferred_element_type=jnp.float32
    ) * (adapter_scale / RERUN_QUERIES)
    gradient_narrow = (
        adapter_scale
        * jnp.dot(gradient_lowered, adapter_up_weight.T, preferred_element_type=jnp.float32)
    ).astype(jnp.bfloat16)
    down_product = lax.dot_general(
        gradient_narrow, context, product_dims, preferred_element_type=jnp.float32
    ) * (1.0 / RERUN_QUERIES)
    return (down_product, up_product)


def local_step(
    queries,
    passages,
    hard_block_offsets,
    positive,
    context,
    residual,
    output_weight,
    adapter_down_weight,
    adapter_up_weight,
    final_norm_weight,
):
    device_count = lax.axis_size(("pb", "pa"))
    block_count, hard_count = hard_block_offsets.shape
    query_count = queries.shape[0]
    block_rows = query_count // block_count
    capacity = 2 * block_count * hard_count // device_count
    slot_width = capacity * block_rows
    slot_rows = device_count * slot_width
    passage_count = passages.shape[0]
    score_scale = inverse_temp / math.sqrt(MODEL_WIDTH)
    own_index = lax.axis_index(("pb", "pa"))
    place = slot_positions(hard_block_offsets, own_index, device_count, capacity, block_rows)
    slot_row = jnp.arange(slot_rows, dtype=jnp.int32)
    sent = slot_row[:, None, None] == place[None]
    sent_row = jnp.any(sent, axis=2)
    outgoing = jnp.dot(
        sent_row.astype(jnp.bfloat16), queries, preferred_element_type=jnp.float32
    ).astype(jnp.bfloat16)
    arrived = exchange(outgoing.reshape(device_count, slot_width, MODEL_WIDTH))
    arrived = arrived.reshape(-1, MODEL_WIDTH)
    whole_weight = lax.all_gather(output_weight, ("pb", "pa"), axis=0, tiled=True)
    near_scores, near_mass, near_mean = partial_softmax(queries, passages, score_scale)
    far_scores, far_mass, far_mean = partial_softmax(arrived, passages, score_scale)
    returned_mass = exchange(far_mass.reshape(device_count, slot_width)).reshape(-1)
    returned_mean = exchange(
        far_mean.astype(jnp.bfloat16).reshape(device_count, slot_width, MODEL_WIDTH)
    )
    returned_mean = returned_mean.reshape(-1, MODEL_WIDTH)
    narrow_projection, hidden_state = layer_hidden(
        context, residual, whole_weight, adapter_down_weight, adapter_up_weight
    )
    held = place[:, :, None] == slot_row[None, None, :]
    own_far_mass = jnp.sum(jnp.where(held, returned_mass[None, None, :], 0.0), axis=2)
    every_mass = jnp.concatenate([near_mass[:, None], own_far_mass], axis=1)
    mass_peak = jnp.max(every_mass, axis=1)
    log_total = mass_peak + jnp.log(jnp.sum(jnp.exp(every_mass - mass_peak[:, None]), axis=1))
    near_share = jnp.exp(near_mass - log_total)
    far_share = jnp.exp(own_far_mass - log_total[:, None])
    log_outgoing = jnp.where(
        jnp.any(sent_row, axis=1),
        jnp.sum(jnp.where(sent_row, log_total[None, :], 0.0), axis=1),
        absent_mass,
    )
    log_arrived = exchange(log_outgoing.reshape(device_count, slot_width)).reshape(-1)
    share_rows = jnp.sum(jnp.where(held, far_share[:, :, None], 0.0), axis=1)
    share_high = lax.reduce_precision(share_rows, 8, 7)
    share_parts = jnp.concatenate([share_high, share_rows - share_high], axis=0)
    mixed_parts = jnp.dot(
        share_parts.astype(jnp.bfloat16), returned_mean, preferred_element_type=jnp.float32
    )
    far_part = mixed_parts[:query_count] + mixed_parts[query_count:]
    positive_hot = positive[:, None] == jnp.arange(passage_count, dtype=jnp.int32)[None, :]
    positive_rows = jnp.dot(
        positive_hot.astype(jnp.bfloat16), passages, preferred_element_type=jnp.float32
    )
    own_part = near_share[:, None] * near_mean - positive_rows
    query_gradient = loss_scale * score_scale * (far_part + own_part)
    far_weight = jnp.exp(far_scores - log_arrived[:, None]).astype(jnp.bfloat16)
    near_weight = (
        jnp.exp(near_scores - log_total[:, None]) - positive_hot.astype(jnp.float32)
    ).astype(jnp.bfloat16)
    product_dims = (((0,), (0,)), ((), ()))
    far_grad = lax.dot_general(
        far_weight, arrived, product_dims, preferred_element_type=jnp.float32
    )
    near_grad = lax.dot_general(
        near_weight, queries, product_dims, preferred_element_type=jnp.float32
    )
    grad_passages = loss_scale * score_scale * (far_grad + near_grad)
    down_product, up_product = layer_parts(
        context,
        narrow_projection,
        hidden_state,
        adapter_up_weight,
        final_norm_weight,
        query_gradient[:RERUN_QUERIES],
    )
    rank = up_product.shape[0]
    adapter_terms = jnp.concatenate([down_product, up_product], axis=0)
    adapter_terms = adapter_terms.reshape(2 * rank, device_count, -1).transpose(1, 0, 2)
    adapter_sums = jnp.sum(exchange(adapter_terms), axis=0)
    return (query_gradient, grad_passages, adapter_sums[:rank].T, adapter_sums[rank:])


def solution(mesh):
    placed = (
        P(("pb", "pa"), None),
        P(("pb", "pa"), None),
        P(("pb", "pa"), None),
        P(("pb", "pa")),
        P(("pb", "pa"), None),
        P(("pb", "pa"), None),
        P(("pb", "pa"), None),
        P(),
        P(),
        P(),
    )
    return jax.shard_map(
        local_step,
        mesh=mesh,
        in_specs=placed,
        out_specs=(
            P(("pb", "pa"), None),
            P(("pb", "pa"), None),
            P(("pb", "pa"), None),
            P(None, ("pb", "pa")),
        ),
        check_vma=False,
    )
```

time: 870 us -> 580 us (0.67); the launches traced: 861 us -> 579 us
  waiting for transfers between devices: 669 us -> 448 us
  local copies, waits for them, and re-layouts: 65.6 us -> 10.7 us
    unnamed x5 -> x1, waiting for transfers between devices: 256 us -> 0.68 us
    gather x7 -> x0, local copies, waits for them, and re-layouts: 35.2 us -> none  [the longest x2 25.2 us: local(): query_blocks[jnp.maximum(slot_block, 0)]]
    all_to_all x4 -> x5, waiting for transfers between devices: 412 us -> 447 us  [exchange(): lax.all_to_all(values, ('pb', 'pa'), split_axis=0, concat_axis=0, tiled=T...]
    reshape x6 -> x2, local copies, waits for them, and re-layouts: 16.7 us -> 4.27 us  [local_step(): adapter_terms.reshape(2 * rank, device_count, -1).transpose(1, 0, 2)]
    dot_general x7 -> x9, matrix products: 49.5 us -> 53.1 us  [the longest x1 20 us: layer_hidden(): jnp.dot(context, whole_weight, preferred_element_type=jnp.float32)]
    all_to_all x4 -> x5, starting transfers between devices: 19.8 us -> 22.5 us  [exchange(): lax.all_to_all(values, ('pb', 'pa'), split_axis=0, concat_axis=0, tiled=T...]
  transfers between devices with their start and end apart: 7 -> 6, of which waited for: 5 -> 4; matrix products, arithmetic and copies ran while one was open for 14% -> 9% of each run, Pallas kernels for 0% -> 0%
where the time goes in v1:
time: 580 us; the launch traced here: 579 us
  waiting for transfers between devices  448 us (77%)
  matrix products  74.9 us (13%)
  starting transfers between devices  22.6 us (4%)
  between operations  14.4 us (2%)
  local copies, waits for them, and re-layouts  10.7 us (2%)
  other arithmetic  9.28 us (2%)
    all_to_all x5, waiting for transfers between devices, exchange(): lax.all_to_all(values, ('pb', 'pa'), split_axis=0, concat_axis=0, tiled=T...  447 us
    all_to_all x5, starting transfers between devices, exchange(): lax.all_to_all(values, ('pb', 'pa'), split_axis=0, concat_axis=0, tiled=T...  22.5 us
    dot_general x1, matrix products, layer_hidden(): jnp.dot(context, whole_weight, preferred_element_type=jnp.float32)  20 us
  transfers between devices with their start and end apart: 6, of which 4 were waited for; matrix products, arithmetic and copies ran while one was open for 9% of the time, Pallas kernels for 0%

profile of v1, /device:TPU:0, one launch (start us, length us, event | category | flops | bytes accessed | tf_op | source)
XLA Modules:
  0.0 579.4 jit_solution(10059192405680812613)
XLA Ops:
  7.2 0.0 copy-start
  7.2 0.0 all-gather.2.cloned.1.call-start
  7.2 0.7 all-gather.2.cloned.1.call-update
  7.9 0.8 copy.24
  8.7 0.1 add.162
  8.8 0.2 convert_reduce_fusion
  9.0 0.1 reduce_sum.93
  9.1 0.1 copy.25
  9.2 0.1 add.168
  9.3 0.1 add.165
  9.4 0.1 add.166
  9.5 0.3 fusion.8
  9.8 5.1 convolution_convert_fusion
  14.9 7.4 %all-to-all-start = ((bf16[32,32,3584]{2,1,0:T(8,128)(2,1)}), bf16[32,32,3584]{2,1,0:T(8,128)(2,1)}, u32[]{:S(2)}, u32[]{:S(2)}) async-start(bf16[32,32,3584]{2,1,0:T(8,128)(2,1)} %bitcast.48), calls=%async_computation | async-start | bytes 14680064 | tf_op jit(solution)/shard_map/all_to_all | solution.py:46
  22.4 3.7 fusion.47
  26.1 278.5 %all-to-all-done = bf16[32,32,3584]{2,1,0:T(8,128)(2,1)} async-done(((bf16[32,32,3584]{2,1,0:T(8,128)(2,1)}), bf16[32,32,3584]{2,1,0:T(8,128)(2,1)}, u32[]{:S(2)}, u32[]{:S(2)}) %all-to-all-start) | async-done | bytes 7340064 | tf_op jit(solution)/shard_map/all_to_all | solution.py:46
  304.6 7.4 %multiply_reduce_fusion.1 = (f32[1024]{0:T(1024)S(1)}, f32[1024,512]{0,1:T(8,128)S(1)}) fusion(bf16[1024,3584]{1,0:T(8,128)(2,1)} %bitcast.1, bf16[512,3584]{1,0:T(8,128)(2,1)} %param.11), kind=kOutput, calls=%fused_computation.29 | convolution fusion | flops 3759143936 | bytes 13111296 | tf_op jit(solution)/shard_map/dot_general | solution.py:34
  312.0 0.4 fusion.11
  312.3 0.9 add.172
  313.2 3.1 all-to-all-start.1
  316.3 0.2 fusion.25
  316.5 6.9 %all-to-all-done.1 = f32[32,1,32]{2,1,0:T(1,128)S(1)} async-done(((f32[32,1,32]{2,1,0:T(1,128)}), f32[32,1,32]{2,1,0:T(1,128)S(1)}, u32[]{:S(2)}, u32[]{:S(2)}) %all-to-all-start.1) | async-done | bytes 4128 | tf_op jit(solution)/shard_map/all_to_all | solution.py:46
  323.4 0.5 broadcast.157
  323.9 0.7 reduce.9
  324.6 0.1 broadcast_in_dim.42
  324.7 0.4 select_reduce_fusion.1
  325.2 0.2 select_reduce_fusion.2
  325.4 0.7 select_n.51
  326.1 2.5 all-to-all-start.3
  328.6 8.2 %divide_convert_fusion = bf16[1024,3584]{1,0:T(8,128)(2,1)} fusion(f32[1024]{0:T(1024)S(1)} %fusion.11, bf16[512,3584]{1,0:T(8,128)(2,1)} %param.11, f32[1024,512]{0,1:T(8,128)S(1)} %get-tuple-element.21, f32[1024]{0:T(1024)S(1)} %get-tuple-element.20), kind=kOutput, calls=%fused_computation | convolution fusion | flops 3767009280 | bytes 13115392 | tf_op jit(solution)/shard_map/dot_general | solution.py:39
  336.8 0.0 all-to-all-done.3
  336.8 0.0 copy-start.11
  336.8 6.1 %all-to-all-start.2 = ((bf16[32,32,3584]{2,1,0:T(8,128)(2,1)}), bf16[32,32,3584]{2,1,0:T(8,128)(2,1)}, u32[]{:S(2)}, u32[]{:S(2)}) async-start(bf16[32,32,3584]{2,1,0:T(8,128)(2,1)} %bitcast.49), calls=%async_computation.2 | async-start | bytes 14680064 | tf_op jit(solution)/shard_map/all_to_all | solution.py:46
  343.0 0.0 copy-start.2
  343.0 3.2 convolution_convert_fusion.1
  346.3 0.3 select_reduce_fusion
  346.6 0.1 reduce-precision_convert_fusion
  346.7 2.0 fusion.7
  348.6 0.7 reduce.10
  349.3 0.1 sub.84
  349.4 156.5 %all-to-all-done.2 = bf16[32,32,3584]{2,1,0:T(8,128)(2,1)} async-done(((bf16[32,32,3584]{2,1,0:T(8,128)(2,1)}), bf16[32,32,3584]{2,1,0:T(8,128)(2,1)}, u32[]{:S(2)}, u32[]{:S(2)}) %all-to-all-start.2) | async-done | bytes 7340064 | tf_op jit(solution)/shard_map/all_to_all | solution.py:46
  505.9 5.3 fusion.20
  511.2 0.9 fusion.6
  512.1 0.0 copy-start.5
  512.2 0.0 copy-start.9
  512.2 0.0 all-gather.2.cloned.1.call-done
  512.2 0.0 copy-start.4
  512.2 20.0 %fusion.48 = f32[512,3584]{1,0:T(8,128)S(1)} fusion(bf16[512,3584]{1,0:T(8,128)(2,1)} %param.14, bf16[3584,3584]{1,0:T(8,128)(2,1)} %all-gather.2.cloned.1.call-done), kind=kOutput, calls=%fused_computation.97 | convolution fusion | flops 13153337344 | bytes 36700160 | tf_op jit(solution)/shard_map/dot_general | solution.py:53
  532.2 2.6 multiply_reduce_fusion
  534.8 2.8 fusion.3
  537.6 0.0 copy-start.1
  537.6 1.8 copy-done.1
  539.4 0.6 convolution_multiply_fusion
  540.0 0.3 copy-done.10
  540.3 5.5 convolution_multiply_fusion.1
  545.8 1.9 pad_maximum_fusion
  547.7 2.1 reshape.260
  549.8 2.1 copy.28
  551.9 3.3 all-to-all-start.4
  555.3 6.3 %fusion.14 = f32[512,3584]{1,0:T(8,128)S(1)} fusion(bf16[1024,3584]{1,0:T(8,128)(2,1)} %bitcast.1, f32[1024,512]{0,1:T(8,128)S(1)} %copy-done.7, f32[1024]{0:T(1024)S(1)} %sub.84), kind=kOutput, calls=%fused_computation.34 | convolution fusion | flops 3759669248 | bytes 16781312 | tf_op jit(solution)/shard_map/dot_general | solution.py:168
  561.6 4.3 add_multiply_fusion
  565.9 5.0 all-to-all-done.4
  570.9 1.1 reduce_sum.102
  572.0 0.6 fusion.46
  (34 shorter events, 0.2 us)
Async XLA Ops:
  7.2 2.7 copy-start
  7.2 505.0 %all-gather.2.cloned.1.call-start = ((), (), s32[]{:S(2)}) async-start(), calls=%async_computation.5 | async-start | bytes 26492928 | tf_op jit(solution)/shard_map/all_gather | solution.py:126
  14.9 289.6 %all-to-all-start = ((bf16[32,32,3584]{2,1,0:T(8,128)(2,1)}), bf16[32,32,3584]{2,1,0:T(8,128)(2,1)}, u32[]{:S(2)}, u32[]{:S(2)}) async-start(bf16[32,32,3584]{2,1,0:T(8,128)(2,1)} %bitcast.48), calls=%async_computation | async-start | bytes 14680064 | tf_op jit(solution)/shard_map/all_to_all | solution.py:46
  312.0 24.9 %copy-start.6 = (f32[1024,512]{0,1:T(8,128)}, f32[1024,512]{0,1:T(8,128)S(1)}, u32[]{:S(2)}) copy-start(f32[1024,512]{0,1:T(8,128)S(1)} %get-tuple-element.21) | copy-start | bytes 6291460
  313.2 10.2 %all-to-all-start.1 = ((f32[32,1,32]{2,1,0:T(1,128)}), f32[32,1,32]{2,1,0:T(1,128)S(1)}, u32[]{:S(2)}, u32[]{:S(2)}) async-start(f32[32,1,32]{2,1,0:T(1,128)} %add.172), calls=%async_computation.1 | async-start | bytes 32768 | tf_op jit(solution)/shard_map/all_to_all | solution.py:46
  326.1 10.7 %all-to-all-start.3 = ((f32[32,1,32]{2,1,0:T(1,128)}), f32[32,1,32]{2,1,0:T(1,128)S(1)}, u32[]{:S(2)}, u32[]{:S(2)}) async-start(f32[32,1,32]{2,1,0:T(1,128)} %select_n.51), calls=%async_computation.3 | async-start | bytes 32768 | tf_op jit(solution)/shard_map/all_to_all | solution.py:46
  336.8 6.2 %copy-start.12 = (bf16[3584]{0:T(1024)(128)(2,1)S(1)}, bf16[3584]{0:T(1024)(128)(2,1)}, u32[]{:S(2)}) copy-start(bf16[3584]{0:T(1024)(128)(2,1)} %param.19) | copy-start | bytes 21508
  336.8 6.2 %copy-start.11 = (bf16[3584,16]{0,1:T(8,128)(2,1)S(1)}, bf16[3584,16]{0,1:T(8,128)(2,1)}, u32[]{:S(2)}) copy-start(bf16[3584,16]{0,1:T(8,128)(2,1)} %param.17) | copy-start | bytes 344068
  336.8 169.0 %all-to-all-start.2 = ((bf16[32,32,3584]{2,1,0:T(8,128)(2,1)}), bf16[32,32,3584]{2,1,0:T(8,128)(2,1)}, u32[]{:S(2)}, u32[]{:S(2)}) async-start(bf16[32,32,3584]{2,1,0:T(8,128)(2,1)} %bitcast.49), calls=%async_computation.2 | async-start | bytes 14680064 | tf_op jit(solution)/shard_map/all_to_all | solution.py:46
  343.0 3.7 copy-start.2
  505.9 5.3 copy-start.3
  505.9 5.3 copy-start.8
  505.9 5.3 copy-start.13
  512.1 20.1 %copy-start.5 = (f32[128,3584]{1,0:T(8,128)}, f32[128,3584]{1,0:T(8,128)S(1)}, u32[]{:S(2)}) copy-start(f32[128,3584]{1,0:T(8,128)S(1)} %fusion.6) | copy-start | bytes 5505028
  512.2 20.0 %copy-start.9 = (bf16[16,3584]{1,0:T(8,128)(2,1)S(1)}, bf16[16,3584]{1,0:T(8,128)(2,1)}, u32[]{:S(2)}) copy-start(bf16[16,3584]{1,0:T(8,128)(2,1)} %param.18) | copy-start | bytes 344068
  512.2 20.0 %copy-start.4 = (bf16[512,3584]{1,0:T(8,128)(2,1)S(1)}, bf16[512,3584]{1,0:T(8,128)(2,1)}, u32[]{:S(2)}) copy-start(bf16[512,3584]{1,0:T(8,128)(2,1)} %param.15) | copy-start | bytes 11010052
  537.6 1.8 copy-start.1
  539.4 0.9 copy-start.10
  545.8 9.5 %copy-start.7 = (f32[1024,512]{0,1:T(8,128)S(1)}, f32[1024,512]{0,1:T(8,128)}, u32[]{:S(2)}) copy-start(f32[1024,512]{0,1:T(8,128)} %copy-done.6) | copy-start | bytes 6291460
  551.9 18.9 %all-to-all-start.4 = ((f32[32,32,112]{2,1,0:T(8,128)}), f32[32,32,112]{2,1,0:T(8,128)}, u32[]{:S(2)}, u32[]{:S(2)}) async-start(f32[32,32,112]{2,1,0:T(8,128)} %bitcast.50), calls=%async_computation.4 | async-start | bytes 1048576 | tf_op jit(solution)/shard_map/all_to_all | solution.py:46
Sparse Core Ops, SparseCore 0:
  10.8 292.8 all-gather.1

commit v2 on v1

--- a/solution.py
+++ b/solution.py
@@ -42,8 +42,43 @@
     return (scores, row_peak + jnp.log(row_mass), row_mean)
 
 
-def exchange(values):
-    return lax.all_to_all(values, ("pb", "pa"), split_axis=0, concat_axis=0, tiled=True)
+def exchange(values, axes):
+    return lax.all_to_all(values, axes, split_axis=0, concat_axis=0, tiled=True)
+
+
+def arrival_table(count):
+    table = []
+    for place in range(count):
+        others = sorted(range(count), key=lambda other: (abs(other - place), other))
+        table.append(others)
+    return table
+
+
+def relay_planes(rows, plane, count):
+    table = arrival_table(count)
+    below, above = [rows], [rows]
+    for step in range(1, count):
+        up = [(i, i + 1) for i in range(step - 1, count - 1)]
+        down = [(i + 1, i) for i in range(count - step)]
+        below.append(lax.ppermute(below[-1], "pb", up))
+        above.append(lax.ppermute(above[-1], "pb", down))
+    chunks = []
+    for order in range(count):
+        source = jnp.array([row[order] for row in table], jnp.int32)[plane]
+        picked = None
+        for place in range(count):
+            shift = place - table[place][order]
+            candidate = below[shift] if shift >= 0 else above[-shift]
+            picked = candidate if picked is None else jnp.where(plane == place, candidate, picked)
+        chunks.append((source, picked))
+    return chunks
+
+
+def chosen(parts, index):
+    result = parts[0]
+    for number in range(1, len(parts)):
+        result = jnp.where(index == number, parts[number], result)
+    return result
 
 
 def layer_hidden(context, residual, whole_weight, adapter_down_weight, adapter_up_weight):
@@ -104,74 +139,125 @@
     adapter_up_weight,
     final_norm_weight,
 ):
-    device_count = lax.axis_size(("pb", "pa"))
+    plane_count, column_count = lax.axis_size("pb"), lax.axis_size("pa")
+    plane, column = lax.axis_index("pb"), lax.axis_index("pa")
+    device_count = plane_count * column_count
     block_count, hard_count = hard_block_offsets.shape
     query_count = queries.shape[0]
     block_rows = query_count // block_count
     capacity = 2 * block_count * hard_count // device_count
     slot_width = capacity * block_rows
     slot_rows = device_count * slot_width
+    plane_rows = column_count * slot_width
     passage_count = passages.shape[0]
     score_scale = inverse_temp / math.sqrt(MODEL_WIDTH)
-    own_index = lax.axis_index(("pb", "pa"))
-    place = slot_positions(hard_block_offsets, own_index, device_count, capacity, block_rows)
+    chunks = relay_planes(queries, plane, plane_count)
+    whole_weight = lax.all_gather(output_weight, ("pb", "pa"), axis=0, tiled=True)
+    plane_places = []
+    for shift in range(plane_count):
+        offsets = hard_block_offsets
+        if shift:
+            offsets = lax.ppermute(
+                offsets, "pb", [(i, (i + shift) % plane_count) for i in range(plane_count)]
+            )
+        source = (plane - shift) % plane_count * column_count + column
+        plane_places.append(
+            slot_positions(offsets, source, device_count, capacity, block_rows)
+        )
+    own_place = plane_places[0]
+    plane_row = jnp.arange(plane_rows, dtype=jnp.int32)
+
+    def plane_hot(source, place=None):
+        if place is None:
+            place = chosen(plane_places, (plane - source) % plane_count)
+        place = place - plane * plane_rows
+        return jnp.any(plane_row[:, None, None] == place[None], axis=2)
+
+    arrived, far_scores, far_mass = [], [], []
+    for order, (source, rows) in enumerate(chunks):
+        packed = jnp.dot(
+            plane_hot(source, None if order else own_place).astype(jnp.bfloat16), rows, preferred_element_type=jnp.float32
+        ).astype(jnp.bfloat16)
+        landed = exchange(packed.reshape(column_count, slot_width, MODEL_WIDTH), "pa")
+        landed = landed.reshape(plane_rows, MODEL_WIDTH)
+        scores = (
+            jnp.dot(landed, passages.T, preferred_element_type=jnp.float32) * score_scale
+        )
+        peak = jnp.max(scores, axis=1)
+        mass = peak + jnp.log(jnp.sum(jnp.exp(scores - peak[:, None]), axis=1))
+        arrived.append(landed)
+        far_scores.append(scores)
+        far_mass.append(mass)
+    near_scores, near_mass, near_mean = partial_softmax(queries, passages, score_scale)
+    orders = jnp.array(
+        [[row.index(p) for p in range(plane_count)] for row in arrival_table(plane_count)],
+        jnp.int32,
+    )[plane]
+    ordered_mass = jnp.stack([chosen(far_mass, orders[p]) for p in range(plane_count)])
+    returned_mass = exchange(
+        ordered_mass.reshape(device_count, slot_width), ("pb", "pa")
+    ).reshape(-1)
     slot_row = jnp.arange(slot_rows, dtype=jnp.int32)
-    sent = slot_row[:, None, None] == place[None]
-    sent_row = jnp.any(sent, axis=2)
-    outgoing = jnp.dot(
-        sent_row.astype(jnp.bfloat16), queries, preferred_element_type=jnp.float32
-    ).astype(jnp.bfloat16)
-    arrived = exchange(outgoing.reshape(device_count, slot_width, MODEL_WIDTH))
-    arrived = arrived.reshape(-1, MODEL_WIDTH)
-    whole_weight = lax.all_gather(output_weight, ("pb", "pa"), axis=0, tiled=True)
-    near_scores, near_mass, near_mean = partial_softmax(queries, passages, score_scale)
-    far_scores, far_mass, far_mean = partial_softmax(arrived, passages, score_scale)
-    returned_mass = exchange(far_mass.reshape(device_count, slot_width)).reshape(-1)
-    returned_mean = exchange(
-        far_mean.astype(jnp.bfloat16).reshape(device_count, slot_width, MODEL_WIDTH)
-    )
-    returned_mean = returned_mean.reshape(-1, MODEL_WIDTH)
-    narrow_projection, hidden_state = layer_hidden(
-        context, residual, whole_weight, adapter_down_weight, adapter_up_weight
-    )
-    held = place[:, :, None] == slot_row[None, None, :]
+    held = own_place[:, :, None] == slot_row[None, None, :]
     own_far_mass = jnp.sum(jnp.where(held, returned_mass[None, None, :], 0.0), axis=2)
     every_mass = jnp.concatenate([near_mass[:, None], own_far_mass], axis=1)
     mass_peak = jnp.max(every_mass, axis=1)
     log_total = mass_peak + jnp.log(jnp.sum(jnp.exp(every_mass - mass_peak[:, None]), axis=1))
     near_share = jnp.exp(near_mass - log_total)
-    far_share = jnp.exp(own_far_mass - log_total[:, None])
+    sent_row = jnp.any(slot_row[:, None, None] == own_place[None], axis=2)
     log_outgoing = jnp.where(
         jnp.any(sent_row, axis=1),
         jnp.sum(jnp.where(sent_row, log_total[None, :], 0.0), axis=1),
         absent_mass,
     )
-    log_arrived = exchange(log_outgoing.reshape(device_count, slot_width)).reshape(-1)
-    share_rows = jnp.sum(jnp.where(held, far_share[:, :, None], 0.0), axis=1)
-    share_high = lax.reduce_precision(share_rows, 8, 7)
-    share_parts = jnp.concatenate([share_high, share_rows - share_high], axis=0)
-    mixed_parts = jnp.dot(
-        share_parts.astype(jnp.bfloat16), returned_mean, preferred_element_type=jnp.float32
-    )
-    far_part = mixed_parts[:query_count] + mixed_parts[query_count:]
+    log_arrived = exchange(
+        log_outgoing.reshape(device_count, slot_width), ("pb", "pa")
+    ).reshape(plane_count, plane_rows)
+    far_weight = []
+    for order, (source, _) in enumerate(chunks):
+        log_rows = chosen([log_arrived[p] for p in range(plane_count)], source)
+        far_weight.append(
+            jnp.exp(far_scores[order] - log_rows[:, None]).astype(jnp.bfloat16)
+        )
+    shifts = sorted(range(plane_count), key=lambda k: -min(k, plane_count - k))
+    far_part = None
+    for shift in shifts:
+        goal = (plane + shift) % plane_count
+        weight_rows = chosen(far_weight, chosen([orders[p] for p in range(plane_count)], goal))
+        share = jnp.dot(weight_rows, passages, preferred_element_type=jnp.float32)
+        share = share.astype(jnp.bfloat16).reshape(column_count, slot_width, MODEL_WIDTH)
+        share = exchange(share, "pa")
+        merged = lax.dot_general(
+            plane_hot(goal, None if shift else own_place).astype(jnp.bfloat16),
+            share.reshape(plane_rows, MODEL_WIDTH),
+            (((0,), (0,)), ((), ())),
+            preferred_element_type=jnp.float32,
+        )
+        if shift:
+            merged = lax.ppermute(
+                merged.astype(jnp.bfloat16),
+                "pb",
+                [(i, (i + shift) % plane_count) for i in range(plane_count)],
+            )
+        far_part = merged.astype(jnp.float32) if far_part is None else far_part + merged.astype(jnp.float32)
+    narrow_projection, hidden_state = layer_hidden(
+        context, residual, whole_weight, adapter_down_weight, adapter_up_weight
+    )
     positive_hot = positive[:, None] == jnp.arange(passage_count, dtype=jnp.int32)[None, :]
     positive_rows = jnp.dot(
         positive_hot.astype(jnp.bfloat16), passages, preferred_element_type=jnp.float32
     )
     own_part = near_share[:, None] * near_mean - positive_rows
     query_gradient = loss_scale * score_scale * (far_part + own_part)
-    far_weight = jnp.exp(far_scores - log_arrived[:, None]).astype(jnp.bfloat16)
     near_weight = (
         jnp.exp(near_scores - log_total[:, None]) - positive_hot.astype(jnp.float32)
     ).astype(jnp.bfloat16)
     product_dims = (((0,), (0,)), ((), ()))
-    far_grad = lax.dot_general(
-        far_weight, arrived, product_dims, preferred_element_type=jnp.float32
-    )
-    near_grad = lax.dot_general(
-        near_weight, queries, product_dims, preferred_element_type=jnp.float32
-    )
-    grad_passages = loss_scale * score_scale * (far_grad + near_grad)
+    every_row = jnp.concatenate([queries] + arrived, axis=0)
+    every_weight = jnp.concatenate([near_weight] + far_weight, axis=0)
+    grad_passages = (loss_scale * score_scale) * lax.dot_general(
+        every_weight, every_row, product_dims, preferred_element_type=jnp.float32
+    )
     down_product, up_product = layer_parts(
         context,
         narrow_projection,
@@ -183,7 +269,9 @@
     rank = up_product.shape[0]
     adapter_terms = jnp.concatenate([down_product, up_product], axis=0)
     adapter_terms = adapter_terms.reshape(2 * rank, device_count, -1).transpose(1, 0, 2)
-    adapter_sums = jnp.sum(exchange(adapter_terms), axis=0)
+    adapter_sums = jnp.sum(
+        exchange(adapter_terms.astype(jnp.bfloat16), ("pb", "pa")).astype(jnp.float32), axis=0
+    )
     return (query_gradient, grad_passages, adapter_sums[:rank].T, adapter_sums[rank:])
 
 

time: 580 us -> 510 us (0.88)
  waiting for transfers between devices: 448 us -> 261 us
  starting transfers between devices: 22.6 us -> 64.8 us
  between operations: 14.4 us -> 40 us
  matrix products: 74.9 us -> 97 us
  local copies, waits for them, and re-layouts: 10.7 us -> 28.5 us
  other arithmetic: 9.28 us -> 16.2 us
    all_to_all x5 -> x11, waiting for transfers between devices: 447 us -> 65.7 us  [exchange(): return lax.all_to_all(values, axes, split_axis=0, concat_axis=0, tiled=True)]
    ppermute x0 -> x12, waiting for transfers between devices: none -> 195 us  [the longest x3 134 us: relay_planes(): above.append(lax.ppermute(above[-1], 'pb', down))]
    dot_general x4 -> x17, matrix products: 21 us -> 57.3 us  [the longest x4 13.6 us: local_step(): jnp.dot(landed, passages.T, preferred_element_type=jnp.float32)]
    ppermute x0 -> x12, starting transfers between devices: none -> 21.7 us  [the longest x3 7.82 us: relay_planes(): below.append(lax.ppermute(below[-1], 'pb', up))]
    all_to_all x5 -> x11, starting transfers between devices: 22.5 us -> 43.1 us  [exchange(): return lax.all_to_all(values, axes, split_axis=0, concat_axis=0, tiled=True)]
    unnamed x29 -> x79, local copies, waits for them, and re-layouts: 2.97 us -> 14.3 us
    dot_general x2 -> x1, matrix products: 10.1 us -> 1.94 us  [partial_softmax(): jnp.dot(weights.astype(jnp.bfloat16), passage_rows, preferred_element_typ...]
    dot_general x2 -> x1, matrix products: 11.1 us -> 3.41 us  [partial_softmax(): jnp.dot(query_rows, passage_rows.T, preferred_element_type=jnp.float32)]
  transfers between devices with their start and end apart: 6 -> 24, of which waited for: 4 -> 13; matrix products, arithmetic and copies ran while one was open for 9% -> 20% of each run, Pallas kernels for 0% -> 0%
where the time goes in v2:
time: 510 us; the launch traced here: 508 us
  waiting for transfers between devices  261 us (51%)
  matrix products  97 us (19%)
  starting transfers between devices  64.8 us (13%)
  between operations  40 us (8%)
  local copies, waits for them, and re-layouts  28.5 us (6%)
  other arithmetic  16.2 us (3%)
    ppermute x3, waiting for transfers between devices, relay_planes(): above.append(lax.ppermute(above[-1], 'pb', down))  134 us
    all_to_all x11, waiting for transfers between devices, exchange(): return lax.all_to_all(values, axes, split_axis=0, concat_axis=0, tiled=True)  65.7 us
    ppermute x3, waiting for transfers between devices, local_step(): lax.ppermute(merged.astype(jnp.bfloat16), 'pb', [(i, (i + shift) % plane_...  60.7 us
    all_to_all x11, starting transfers between devices, exchange(): return lax.all_to_all(values, axes, split_axis=0, concat_axis=0, tiled=True)  43.1 us
    dot_general x1, matrix products, layer_hidden(): jnp.dot(context, whole_weight, preferred_element_type=jnp.float32)  19.9 us
    unnamed x79, local copies, waits for them, and re-layouts  14.3 us
    dot_general x4, matrix products, local_step(): jnp.dot(landed, passages.T, preferred_element_type=jnp.float32)  13.6 us
    dot_general x4, matrix products, local_step(): jnp.dot(plane_hot(source, None if order else own_place).astype(jnp.bfloat...  12.5 us
  transfers between devices with their start and end apart: 24, of which 13 were waited for; matrix products, arithmetic and copies ran while one was open for 20% of the time, Pallas kernels for 0%

profile of v2, /device:TPU:0, one launch (start us, length us, event | category | flops | bytes accessed | tf_op | source)
XLA Modules:
  0.0 507.8 jit_solution(14010958043551562745)
XLA Ops:
  8.7 3.1 collective-permute-start.2
  11.7 2.6 collective-permute-start.1
  14.3 1.3 collective-permute-start
  17.6 1.3 dynamic_slice.17
  25.3 3.0 convolution_convert_fusion
  28.3 3.7 all-to-all-start.3
  32.0 1.3 collective-permute-start.6
  33.3 5.5 %collective-permute-start.3 = (bf16[128,3584]{1,0:T(8,128)(2,1)S(1)}, bf16[128,3584]{1,0:T(8,128)(2,1)}, u32[]{:S(2)}, u32[]{:S(2)}) collective-permute-start(bf16[128,3584]{1,0:T(8,128)(2,1)S(1)} %copy-done.8), channel_id=1, source_target_pairs={{0,8},{8,16},{16,24},{1,9},{9,17},{17,25},{2,10},{10,18},{18,26},{... | collective-permute-start | bytes 2752520 | tf_op jit(solution)/shard_map/ppermute | solution.py:63
  38.9 31.9 %collective-permute-done.6 = bf16[128,3584]{1,0:T(8,128)(2,1)} collective-permute-done((bf16[128,3584]{1,0:T(8,128)(2,1)S(1)}, bf16[128,3584]{1,0:T(8,128)(2,1)}, u32[]{:S(2)}, u32[]{:S(2)}) %collective-permute-start.6) | collective-permute-done | bytes 917536 | tf_op jit(solution)/shard_map/ppermute | solution.py:64
  70.8 3.3 convolution_convert_fusion.1
  74.2 4.3 all-to-all-start.2
  80.6 45.4 %collective-permute-done.7 = bf16[128,3584]{1,0:T(8,128)(2,1)S(1)} collective-permute-done((bf16[128,3584]{1,0:T(8,128)(2,1)}, bf16[128,3584]{1,0:T(8,128)(2,1)S(1)}, u32[]{:S(2)}, u32[]{:S(2)}) %collective-permute-start.7) | collective-permute-done | bytes 917536 | tf_op jit(solution)/shard_map/ppermute | solution.py:64
  127.9 3.1 convolution_convert_fusion.2
  131.0 4.3 all-to-all-start.1
  136.6 1.6 collective-permute-start.5
  144.9 3.4 fusion.98
  148.4 56.8 %collective-permute-done.8 = bf16[128,3584]{1,0:T(8,128)(2,1)} collective-permute-done((bf16[128,3584]{1,0:T(8,128)(2,1)}, bf16[128,3584]{1,0:T(8,128)(2,1)}, u32[]{:S(2)}, u32[]{:S(2)}) %collective-permute-start.8) | collective-permute-done | bytes 917536 | tf_op jit(solution)/shard_map/ppermute | solution.py:64
  205.2 3.1 convolution_convert_fusion.3
  208.3 4.3 all-to-all-start
  223.3 3.4 fusion.99
  226.8 2.9 fusion.100
  230.8 3.4 fusion.101
  234.2 2.2 all-to-all-done
  236.4 3.9 fusion.102
  241.9 3.2 all-to-all-start.4
  245.3 6.9 %all-to-all-done.4 = f32[32,1,32]{2,1,0:T(1,128)S(1)} async-done(((f32[32,1,32]{2,1,0:T(1,128)}), f32[32,1,32]{2,1,0:T(1,128)S(1)}, u32[]{:S(2)}, u32[]{:S(2)}) %all-to-all-start.4) | async-done | bytes 4128 | tf_op jit(solution)/shard_map/all_to_all | solution.py:46
  255.5 2.7 all-to-all-start.5
  259.1 6.4 %all-to-all-done.5 = f32[32,1,32]{2,1,0:T(1,128)S(1)} async-done(((f32[32,1,32]{2,1,0:T(1,128)}), f32[32,1,32]{2,1,0:T(1,128)S(1)}, u32[]{:S(2)}, u32[]{:S(2)}) %all-to-all-start.5) | async-done | bytes 4128 | tf_op jit(solution)/shard_map/all_to_all | solution.py:46
  265.8 2.1 constant_dynamic-update-slice_fusion.3
  267.9 1.9 constant_dynamic-update-slice_fusion.2
  269.8 1.9 constant_dynamic-update-slice_fusion.1
  271.7 2.0 constant_dynamic-update-slice_fusion
  273.7 2.4 convolution_convert_fusion.5
  276.1 4.3 all-to-all-start.8
  287.9 4.4 convolution_convert_fusion.6
  292.3 11.9 %all-to-all-done.8 = bf16[8,32,3584]{2,1,0:T(8,128)(2,1)} async-done(((bf16[8,32,3584]{2,1,0:T(8,128)(2,1)}), bf16[8,32,3584]{2,1,0:T(8,128)(2,1)}, u32[]{:S(2)}, u32[]{:S(2)}) %all-to-all-start.8) | async-done | bytes 1835040 | tf_op jit(solution)/shard_map/all_to_all | solution.py:46
  304.2 4.3 all-to-all-start.7
  308.6 3.2 convolution_convert_fusion.11
  313.1 2.4 convolution_convert_fusion.7
  315.5 16.8 %all-to-all-done.7 = bf16[8,32,3584]{2,1,0:T(8,128)(2,1)} async-done(((bf16[8,32,3584]{2,1,0:T(8,128)(2,1)}), bf16[8,32,3584]{2,1,0:T(8,128)(2,1)}, u32[]{:S(2)}, u32[]{:S(2)}) %all-to-all-start.7) | async-done | bytes 1835040 | tf_op jit(solution)/shard_map/all_to_all | solution.py:46
  332.3 4.3 all-to-all-start.6
  336.7 1.4 constant_dynamic-update-slice_fusion.7
  338.0 3.1 constant_dynamic-update-slice_fusion.6
  341.1 2.8 constant_dynamic-update-slice_fusion.5
  344.0 2.4 convolution_convert_fusion.4
  346.4 14.1 %all-to-all-done.6 = bf16[8,32,3584]{2,1,0:T(8,128)(2,1)} async-done(((bf16[8,32,3584]{2,1,0:T(8,128)(2,1)}), bf16[8,32,3584]{2,1,0:T(8,128)(2,1)}, u32[]{:S(2)}, u32[]{:S(2)}) %all-to-all-start.6) | async-done | bytes 1835040 | tf_op jit(solution)/shard_map/all_to_all | solution.py:46
  360.5 3.6 all-to-all-start.9
  364.1 2.9 convolution_convert_fusion.8
  367.5 2.9 convolution_convert_fusion.10
  370.5 1.5 collective-permute-start.9
  372.0 2.9 convolution_convert_fusion.9
  375.8 2.8 constant_dynamic-update-slice_fusion.4
  378.7 1.9 fusion.5
  380.6 7.2 %all-to-all-done.9 = bf16[8,32,3584]{2,1,0:T(8,128)(2,1)S(1)} async-done(((bf16[8,32,3584]{2,1,0:T(8,128)(2,1)}), bf16[8,32,3584]{2,1,0:T(8,128)(2,1)S(1)}, u32[]{:S(2)}, u32[]{:S(2)}) %all-to-all-start.9) | async-done | bytes 1835040 | tf_op jit(solution)/shard_map/all_to_all | solution.py:46
  388.3 1.8 collective-permute-done.11
  390.0 58.9 %collective-permute-done.9 = bf16[128,3584]{1,0:T(8,128)(2,1)} collective-permute-done((bf16[128,3584]{1,0:T(8,128)(2,1)}, bf16[128,3584]{1,0:T(8,128)(2,1)}, u32[]{:S(2)}, u32[]{:S(2)}) %collective-permute-start.9) | collective-permute-done | bytes 917536 | tf_op jit(solution)/shard_map/ppermute | solution.py:237
  449.0 3.2 add_multiply_fusion
  452.2 19.9 %fusion.104 = f32[512,3584]{1,0:T(8,128)S(1)} fusion(bf16[512,3584]{1,0:T(8,128)(2,1)} %param.19, bf16[3584,3584]{1,0:T(8,128)(2,1)} %all-gather.2.cloned.1.call-done), kind=kOutput, calls=%fused_computation.241 | convolution fusion | flops 13153337344 | bytes 36700160 | tf_op jit(solution)/shard_map/dot_general | solution.py:88
  472.2 2.6 multiply_reduce_fusion
  474.8 2.5 fusion.3
  477.4 1.8 copy-done.7
  479.8 4.9 fusion.6
  485.8 3.9 all-to-all-start.10
  489.7 10.4 %convolution_multiply_fusion = f32[512,3584]{1,0:T(8,128)} fusion(bf16[1152,512]{1,0:T(8,128)(2,1)S(1)} %copy-done.27, bf16[1152,3584]{1,0:T(8,128)(2,1)} %constant_dynamic-update-slice_fusion.4), kind=kOutput, calls=%fused_computation.8 | convolution fusion | flops 4229693440 | bytes 16777216 | tf_op jit(solution)/shard_map/dot_general | solution.py:258
  (183 shorter events, 27.9 us)
Async XLA Ops:
  7.2 465.0 %copy-start = (bf16[16,3584]{1,0:T(8,128)(2,1)S(1)}, bf16[16,3584]{1,0:T(8,128)(2,1)}, u32[]{:S(2)}) copy-start(bf16[16,3584]{1,0:T(8,128)(2,1)} %param.23) | copy-start | bytes 344068
  7.2 445.0 %all-gather.2.cloned.1.call-start = ((), (), s32[]{:S(2)}) async-start(), calls=%async_computation.11 | async-start | bytes 26492928 | tf_op jit(solution)/shard_map/all_gather | solution.py:155
  8.7 13.7 %collective-permute-start.2 = (s32[32,4]{1,0:T(8,128)S(1)}, s32[32,4]{1,0:T(8,128)S(1)}, u32[]{:S(2)}, u32[]{:S(2)}) collective-permute-start(s32[32,4]{1,0:T(8,128)S(1)} %copy.43), channel_id=1, source_target_pairs={{0,8},{8,16},{16,24},{24,0},{1,9},{9,17},{17,25},{25,1},{2,10},{10... | collective-permute-start | bytes 1544 | tf_op jit(solution)/shard_map/ppermute | solution.py:160
  11.7 11.1 %collective-permute-start.1 = (s32[32,4]{1,0:T(8,128)S(1)}, s32[32,4]{1,0:T(8,128)S(1)}, u32[]{:S(2)}, u32[]{:S(2)}) collective-permute-start(s32[32,4]{1,0:T(8,128)S(1)} %copy.43), channel_id=1, source_target_pairs={{0,16},{8,24},{16,0},{24,8},{1,17},{9,25},{17,1},{25,9},{2,18},{10... | collective-permute-start | bytes 1544 | tf_op jit(solution)/shard_map/ppermute | solution.py:160
  14.3 9.2 %collective-permute-start = (s32[32,4]{1,0:T(8,128)S(1)}, s32[32,4]{1,0:T(8,128)S(1)}, u32[]{:S(2)}, u32[]{:S(2)}) collective-permute-start(s32[32,4]{1,0:T(8,128)S(1)} %copy.43), channel_id=1, source_target_pairs={{0,24},{8,0},{16,8},{24,16},{1,25},{9,1},{17,9},{25,17},{2,26},{10... | collective-permute-start | bytes 1544 | tf_op jit(solution)/shard_map/ppermute | solution.py:160
  22.4 9.6 %copy-start.8 = (bf16[128,3584]{1,0:T(8,128)(2,1)S(1)}, bf16[128,3584]{1,0:T(8,128)(2,1)}, u32[]{:S(2)}) copy-start(bf16[128,3584]{1,0:T(8,128)(2,1)} %param.15) | copy-start | bytes 2752516
  28.3 45.9 %all-to-all-start.3 = ((bf16[8,32,3584]{2,1,0:T(8,128)(2,1)}), bf16[8,32,3584]{2,1,0:T(8,128)(2,1)S(1)}, u32[]{:S(2)}, u32[]{:S(2)}) async-start(bf16[8,32,3584]{2,1,0:T(8,128)(2,1)} %bitcast.105), calls=%async_computation.3 | async-start | bytes 3670016 | tf_op jit(solution)/shard_map/all_to_all | solution.py:46
  32.0 38.8 %collective-permute-start.6 = (bf16[128,3584]{1,0:T(8,128)(2,1)S(1)}, bf16[128,3584]{1,0:T(8,128)(2,1)}, u32[]{:S(2)}, u32[]{:S(2)}) collective-permute-start(bf16[128,3584]{1,0:T(8,128)(2,1)S(1)} %copy-done.8), channel_id=1, source_target_pairs={{8,0},{16,8},{24,16},{9,1},{17,9},{25,17},{10,2},{18,10},{26,18},{... | collective-permute-start | bytes 2752520 | tf_op jit(solution)/shard_map/ppermute | solution.py:64
  33.3 37.5 %collective-permute-start.3 = (bf16[128,3584]{1,0:T(8,128)(2,1)S(1)}, bf16[128,3584]{1,0:T(8,128)(2,1)}, u32[]{:S(2)}, u32[]{:S(2)}) collective-permute-start(bf16[128,3584]{1,0:T(8,128)(2,1)S(1)} %copy-done.8), channel_id=1, source_target_pairs={{0,8},{8,16},{16,24},{1,9},{9,17},{17,25},{2,10},{10,18},{18,26},{... | collective-permute-start | bytes 2752520 | tf_op jit(solution)/shard_map/ppermute | solution.py:63
  74.2 56.8 %all-to-all-start.2 = ((bf16[8,32,3584]{2,1,0:T(8,128)(2,1)}), bf16[8,32,3584]{2,1,0:T(8,128)(2,1)}, u32[]{:S(2)}, u32[]{:S(2)}) async-start(bf16[8,32,3584]{2,1,0:T(8,128)(2,1)} %bitcast.106), calls=%async_computation.2 | async-start | bytes 3670016 | tf_op jit(solution)/shard_map/all_to_all | solution.py:46
  78.5 47.5 %collective-permute-start.7 = (bf16[128,3584]{1,0:T(8,128)(2,1)}, bf16[128,3584]{1,0:T(8,128)(2,1)S(1)}, u32[]{:S(2)}, u32[]{:S(2)}) collective-permute-start(bf16[128,3584]{1,0:T(8,128)(2,1)} %collective-permute-done.6), channel_id=1, source_target_pairs={{8,0},{16,8},{9,1},{17,9},{10,2},{18,10},{11,3},{19,11},{12,4},{20... | collective-permute-start | bytes 2752520 | tf_op jit(solution)/shard_map/ppermute | solution.py:64
  79.8 46.2 %collective-permute-start.4 = (bf16[128,3584]{1,0:T(8,128)(2,1)}, bf16[128,3584]{1,0:T(8,128)(2,1)S(1)}, u32[]{:S(2)}, u32[]{:S(2)}) collective-permute-start(bf16[128,3584]{1,0:T(8,128)(2,1)} %collective-permute-done.3), channel_id=1, source_target_pairs={{8,16},{16,24},{9,17},{17,25},{10,18},{18,26},{11,19},{19,27},{12,... | collective-permute-start | bytes 2752520 | tf_op jit(solution)/shard_map/ppermute | solution.py:63
  126.0 1.0 copy-start.15
  127.0 0.9 copy-start.17
  131.0 77.3 %all-to-all-start.1 = ((bf16[8,32,3584]{2,1,0:T(8,128)(2,1)}), bf16[8,32,3584]{2,1,0:T(8,128)(2,1)}, u32[]{:S(2)}, u32[]{:S(2)}) async-start(bf16[8,32,3584]{2,1,0:T(8,128)(2,1)} %bitcast.100), calls=%async_computation.1 | async-start | bytes 3670016 | tf_op jit(solution)/shard_map/all_to_all | solution.py:46
  135.3 69.8 %collective-permute-start.8 = (bf16[128,3584]{1,0:T(8,128)(2,1)}, bf16[128,3584]{1,0:T(8,128)(2,1)}, u32[]{:S(2)}, u32[]{:S(2)}) collective-permute-start(bf16[128,3584]{1,0:T(8,128)(2,1)} %copy-done.15), channel_id=1, source_target_pairs={{8,0},{9,1},{10,2},{11,3},{12,4},{13,5},{14,6},{15,7}} | collective-permute-start | bytes 2752520 | tf_op jit(solution)/shard_map/ppermute | solution.py:64
  136.6 68.5 %collective-permute-start.5 = (bf16[128,3584]{1,0:T(8,128)(2,1)}, bf16[128,3584]{1,0:T(8,128)(2,1)}, u32[]{:S(2)}, u32[]{:S(2)}) collective-permute-start(bf16[128,3584]{1,0:T(8,128)(2,1)} %copy-done.17), channel_id=1, source_target_pairs={{16,24},{17,25},{18,26},{19,27},{20,28},{21,29},{22,30},{23,31}} | collective-permute-start | bytes 2752520 | tf_op jit(solution)/shard_map/ppermute | solution.py:63
  144.0 61.1 %copy-start.16 = (bf16[128,3584]{1,0:T(8,128)(2,1)S(1)}, bf16[128,3584]{1,0:T(8,128)(2,1)}, u32[]{:S(2)}) copy-start(bf16[128,3584]{1,0:T(8,128)(2,1)} %copy-done.15) | copy-start | bytes 2752516
  144.0 61.1 %copy-start.18 = (bf16[128,3584]{1,0:T(8,128)(2,1)S(1)}, bf16[128,3584]{1,0:T(8,128)(2,1)}, u32[]{:S(2)}) copy-start(bf16[128,3584]{1,0:T(8,128)(2,1)} %copy-done.17) | copy-start | bytes 2752516
  148.3 105.8 %copy-start.28 = (f32[128]{0:T(128)}, f32[128]{0:T(128)S(1)}, u32[]{:S(2)}) copy-start(f32[128]{0:T(128)S(1)} %get-tuple-element.47) | copy-start | bytes 1540
  148.3 110.0 %copy-start.20 = (f32[128,512]{1,0:T(8,128)}, f32[128,512]{1,0:T(8,128)S(1)}, u32[]{:S(2)}) copy-start(f32[128,512]{1,0:T(8,128)S(1)} %get-tuple-element.48) | copy-start | bytes 786436
  208.3 28.1 %all-to-all-start = ((bf16[8,32,3584]{2,1,0:T(8,128)(2,1)}), bf16[8,32,3584]{2,1,0:T(8,128)(2,1)}, u32[]{:S(2)}, u32[]{:S(2)}) async-start(bf16[8,32,3584]{2,1,0:T(8,128)(2,1)} %bitcast.101), calls=%async_computation | async-start | bytes 3670016 | tf_op jit(solution)/shard_map/all_to_all | solution.py:46
  223.1 3.6 copy-start.1
  223.3 30.8 %copy-start.32 = (f32[128]{0:T(128)}, f32[128]{0:T(128)S(1)}, u32[]{:S(2)}) copy-start(f32[128]{0:T(128)S(1)} %fusion.57) | copy-start | bytes 1540
  226.7 4.0 copy-start.25
  229.7 0.8 copy-start.23
  236.4 3.9 copy-start.24
  236.4 21.8 %copy-start.34 = (s32[128]{0:T(128)S(1)}, s32[128]{0:T(128)}, u32[]{:S(2)}) copy-start(s32[128]{0:T(128)} %param.18) | copy-start | bytes 1540
  240.3 0.8 copy-start.26
  241.9 10.4 %all-to-all-start.4 = ((f32[32,1,32]{2,1,0:T(1,128)}), f32[32,1,32]{2,1,0:T(1,128)S(1)}, u32[]{:S(2)}, u32[]{:S(2)}) async-start(f32[32,1,32]{2,1,0:T(1,128)} %all_to_all.41), calls=%async_computation.4 | async-start | bytes 32768 | tf_op jit(solution)/shard_map/all_to_all | solution.py:46
  255.5 9.9 %all-to-all-start.5 = ((f32[32,1,32]{2,1,0:T(1,128)}), f32[32,1,32]{2,1,0:T(1,128)S(1)}, u32[]{:S(2)}, u32[]{:S(2)}) async-start(f32[32,1,32]{2,1,0:T(1,128)} %select_n.895), calls=%async_computation.5 | async-start | bytes 32768 | tf_op jit(solution)/shard_map/all_to_all | solution.py:46
  265.8 7.8 %copy-start.2 = (bf16[512,3584]{1,0:T(8,128)(2,1)S(1)}, bf16[512,3584]{1,0:T(8,128)(2,1)}, u32[]{:S(2)}) copy-start(bf16[512,3584]{1,0:T(8,128)(2,1)} %param.16) | copy-start | bytes 11010052
  271.7 4.4 copy-start.9
  273.7 2.4 copy-start.12
  273.7 14.2 %copy-start.30 = (bf16[3584]{0:T(1024)(128)(2,1)S(1)}, bf16[3584]{0:T(1024)(128)(2,1)}, u32[]{:S(2)}) copy-start(bf16[3584]{0:T(1024)(128)(2,1)} %param.24) | copy-start | bytes 21508
  276.1 28.1 %all-to-all-start.8 = ((bf16[8,32,3584]{2,1,0:T(8,128)(2,1)}), bf16[8,32,3584]{2,1,0:T(8,128)(2,1)}, u32[]{:S(2)}, u32[]{:S(2)}) async-start(bf16[8,32,3584]{2,1,0:T(8,128)(2,1)} %bitcast.99), calls=%async_computation.8 | async-start | bytes 3670016 | tf_op jit(solution)/shard_map/all_to_all | solution.py:46
  304.2 28.1 %all-to-all-start.7 = ((bf16[8,32,3584]{2,1,0:T(8,128)(2,1)}), bf16[8,32,3584]{2,1,0:T(8,128)(2,1)}, u32[]{:S(2)}, u32[]{:S(2)}) async-start(bf16[8,32,3584]{2,1,0:T(8,128)(2,1)} %bitcast.103), calls=%async_computation.7 | async-start | bytes 3670016 | tf_op jit(solution)/shard_map/all_to_all | solution.py:46
  308.5 4.5 copy-start.31
  308.5 4.6 copy-start.3
  308.5 4.6 copy-start.10
  308.6 4.6 copy-start.13
  332.3 28.1 %all-to-all-start.6 = ((bf16[8,32,3584]{2,1,0:T(8,128)(2,1)}), bf16[8,32,3584]{2,1,0:T(8,128)(2,1)}, u32[]{:S(2)}, u32[]{:S(2)}) async-start(bf16[8,32,3584]{2,1,0:T(8,128)(2,1)} %bitcast.104), calls=%async_computation.6 | async-start | bytes 3670016 | tf_op jit(solution)/shard_map/all_to_all | solution.py:46
  338.0 6.0 %copy-start.4 = (bf16[512,3584]{1,0:T(8,128)(2,1)S(1)}, bf16[512,3584]{1,0:T(8,128)(2,1)}, u32[]{:S(2)}) copy-start(bf16[512,3584]{1,0:T(8,128)(2,1)} %param.16) | copy-start | bytes 11010052
  338.0 6.0 %copy-start.11 = (bf16[256,512]{1,0:T(8,128)(2,1)S(1)}, bf16[256,512]{1,0:T(8,128)(2,1)}, u32[]{:S(2)}) copy-start(bf16[256,512]{1,0:T(8,128)(2,1)} %copy-done.9) | copy-start | bytes 786436
  338.0 6.0 %copy-start.14 = (bf16[256,512]{1,0:T(8,128)(2,1)S(1)}, bf16[256,512]{1,0:T(8,128)(2,1)}, u32[]{:S(2)}) copy-start(bf16[256,512]{1,0:T(8,128)(2,1)} %copy-done.12) | copy-start | bytes 786436
  360.5 27.3 %all-to-all-start.9 = ((bf16[8,32,3584]{2,1,0:T(8,128)(2,1)}), bf16[8,32,3584]{2,1,0:T(8,128)(2,1)S(1)}, u32[]{:S(2)}, u32[]{:S(2)}) async-start(bf16[8,32,3584]{2,1,0:T(8,128)(2,1)} %bitcast.102), calls=%async_computation.9 | async-start | bytes 3670016 | tf_op jit(solution)/shard_map/all_to_all | solution.py:46
  367.0 23.1 %collective-permute-start.11 = (bf16[128,3584]{1,0:T(8,128)(2,1)}, bf16[128,3584]{1,0:T(8,128)(2,1)S(1)}, u32[]{:S(2)}, u32[]{:S(2)}) collective-permute-start(bf16[128,3584]{1,0:T(8,128)(2,1)} %convolution_convert_fusion.8), channel_id=1, source_target_pairs={{0,24},{8,0},{16,8},{24,16},{1,25},{9,1},{17,9},{25,17},{2,26},{10... | collective-permute-start | bytes 2752520 | tf_op jit(solution)/shard_map/ppermute | solution.py:237
  370.4 8.2 %copy-start.5 = (bf16[512,3584]{1,0:T(8,128)(2,1)S(1)}, bf16[512,3584]{1,0:T(8,128)(2,1)}, u32[]{:S(2)}) copy-start(bf16[512,3584]{1,0:T(8,128)(2,1)} %param.16) | copy-start | bytes 11010052
  370.4 8.2 %copy-start.21 = (f32[128,512]{1,0:T(8,128)S(1)}, f32[128,512]{1,0:T(8,128)}, u32[]{:S(2)}) copy-start(f32[128,512]{1,0:T(8,128)} %copy-done.20) | copy-start | bytes 786436
  370.4 8.2 %copy-start.29 = (f32[128]{0:T(128)S(1)}, f32[128]{0:T(128)}, u32[]{:S(2)}) copy-start(f32[128]{0:T(128)} %copy-done.28) | copy-start | bytes 1540
  370.4 8.2 %copy-start.33 = (f32[128]{0:T(128)S(1)}, f32[128]{0:T(128)}, u32[]{:S(2)}) copy-start(f32[128]{0:T(128)} %copy-done.32) | copy-start | bytes 1540
  370.4 8.2 %copy-start.36 = (f32[128]{0:T(128)S(1)}, f32[128]{0:T(128)}, u32[]{:S(2)}) copy-start(f32[128]{0:T(128)} %get-tuple-element.20) | copy-start | bytes 1540
  370.5 78.5 %collective-permute-start.9 = (bf16[128,3584]{1,0:T(8,128)(2,1)}, bf16[128,3584]{1,0:T(8,128)(2,1)}, u32[]{:S(2)}, u32[]{:S(2)}) collective-permute-start(bf16[128,3584]{1,0:T(8,128)(2,1)} %convolution_convert_fusion.10), channel_id=1, source_target_pairs={{0,16},{8,24},{16,0},{24,8},{1,17},{9,25},{17,1},{25,9},{2,18},{10... | collective-permute-start | bytes 2752520 | tf_op jit(solution)/shard_map/ppermute | solution.py:237
  374.9 74.0 %collective-permute-start.10 = (bf16[128,3584]{1,0:T(8,128)(2,1)}, bf16[128,3584]{1,0:T(8,128)(2,1)}, u32[]{:S(2)}, u32[]{:S(2)}) collective-permute-start(bf16[128,3584]{1,0:T(8,128)(2,1)} %convolution_convert_fusion.9), channel_id=1, source_target_pairs={{0,8},{8,16},{16,24},{24,0},{1,9},{9,17},{17,25},{25,1},{2,10},{10... | collective-permute-start | bytes 2752520 | tf_op jit(solution)/shard_map/ppermute | solution.py:237
  380.6 68.3 %copy-start.35 = (s32[128]{0:T(128)S(1)}, s32[128]{0:T(128)}, u32[]{:S(2)}) copy-start(s32[128]{0:T(128)} %param.18) | copy-start | bytes 1540
  387.8 61.1 %copy-start.6 = (bf16[512,3584]{1,0:T(8,128)(2,1)S(1)}, bf16[512,3584]{1,0:T(8,128)(2,1)}, u32[]{:S(2)}) copy-start(bf16[512,3584]{1,0:T(8,128)(2,1)} %param.16) | copy-start | bytes 11010052
  452.2 20.0 %copy-start.22 = (f32[128,3584]{1,0:T(8,128)}, f32[128,3584]{1,0:T(8,128)S(1)}, u32[]{:S(2)}) copy-start(f32[128,3584]{1,0:T(8,128)S(1)} %add_multiply_fusion) | copy-start | bytes 5505028
  452.2 20.0 %copy-start.19 = (bf16[512,3584]{1,0:T(8,128)(2,1)S(1)}, bf16[512,3584]{1,0:T(8,128)(2,1)}, u32[]{:S(2)}) copy-start(bf16[512,3584]{1,0:T(8,128)(2,1)} %param.20) | copy-start | bytes 11010052
  477.4 1.8 copy-start.7
  479.8 9.9 %copy-start.27 = (bf16[1152,512]{1,0:T(8,128)(2,1)S(1)}, bf16[1152,512]{1,0:T(8,128)(2,1)}, u32[]{:S(2)}) copy-start(bf16[1152,512]{1,0:T(8,128)(2,1)} %get-tuple-element.12) | copy-start | bytes 3538948
  485.8 14.4 %all-to-all-start.10 = ((bf16[32,32,112]{2,1,0:T(8,128)(2,1)}), bf16[32,32,112]{2,1,0:T(8,128)(2,1)S(1)}, u32[]{:S(2)}, u32[]{:S(2)}) async-start(bf16[32,32,112]{2,1,0:T(8,128)(2,1)} %bitcast.95), calls=%async_computation.10 | async-start | bytes 524288 | tf_op jit(solution)/shard_map/all_to_all | solution.py:46
Sparse Core Ops, SparseCore 0:
  10.8 194.9 all-gather.1

commit v3 on v2

--- a/solution.py
+++ b/solution.py
@@ -64,7 +64,7 @@
         above.append(lax.ppermute(above[-1], "pb", down))
     chunks = []
     for order in range(count):
-        source = jnp.array([row[order] for row in table], jnp.int32)[plane]
+        source = chosen([jnp.int32(row[order]) for row in table], plane)
         picked = None
         for place in range(count):
             shift = place - table[place][order]
@@ -189,10 +189,10 @@
         far_scores.append(scores)
         far_mass.append(mass)
     near_scores, near_mass, near_mean = partial_softmax(queries, passages, score_scale)
-    orders = jnp.array(
-        [[row.index(p) for p in range(plane_count)] for row in arrival_table(plane_count)],
-        jnp.int32,
-    )[plane]
+    table = arrival_table(plane_count)
+    orders = [
+        chosen([jnp.int32(row.index(p)) for row in table], plane) for p in range(plane_count)
+    ]
     ordered_mass = jnp.stack([chosen(far_mass, orders[p]) for p in range(plane_count)])
     returned_mass = exchange(
         ordered_mass.reshape(device_count, slot_width), ("pb", "pa")
@@ -223,7 +223,7 @@
     far_part = None
     for shift in shifts:
         goal = (plane + shift) % plane_count
-        weight_rows = chosen(far_weight, chosen([orders[p] for p in range(plane_count)], goal))
+        weight_rows = chosen(far_weight, chosen(orders, goal))
         share = jnp.dot(weight_rows, passages, preferred_element_type=jnp.float32)
         share = share.astype(jnp.bfloat16).reshape(column_count, slot_width, MODEL_WIDTH)
         share = exchange(share, "pa")

time: 510 us -> 492 us (0.965)
  between operations: 40 us -> 15 us
  waiting for transfers between devices: 261 us -> 276 us
    all_to_all x11, waiting for transfers between devices: 65.7 us -> 79.7 us  [exchange(): return lax.all_to_all(values, axes, split_axis=0, concat_axis=0, tiled=True)]
  transfers between devices with their start and end apart: 24 -> 24, of which waited for: 13 -> 14; matrix products, arithmetic and copies ran while one was open for 20% -> 20% of each run, Pallas kernels for 0% -> 0%
where the time goes in v3:
time: 492 us; the launch traced here: 490 us
  waiting for transfers between devices  276 us (56%)
  matrix products  94.6 us (19%)
  starting transfers between devices  63.1 us (13%)
  local copies, waits for them, and re-layouts  25.1 us (5%)
  other arithmetic  16.2 us (3%)
  between operations  15 us (3%)
    ppermute x3, waiting for transfers between devices, relay_planes(): above.append(lax.ppermute(above[-1], 'pb', down))  135 us
    all_to_all x11, waiting for transfers between devices, exchange(): return lax.all_to_all(values, axes, split_axis=0, concat_axis=0, tiled=True)  79.7 us
    ppermute x3, waiting for transfers between devices, local_step(): lax.ppermute(merged.astype(jnp.bfloat16), 'pb', [(i, (i + shift) % plane_...  60.7 us
    all_to_all x11, starting transfers between devices, exchange(): return lax.all_to_all(values, axes, split_axis=0, concat_axis=0, tiled=True)  43.1 us
    dot_general x1, matrix products, layer_hidden(): jnp.dot(context, whole_weight, preferred_element_type=jnp.float32)  19.9 us
    unnamed x79, local copies, waits for them, and re-layouts  16.2 us
    dot_general x4, matrix products, local_step(): jnp.dot(landed, passages.T, preferred_element_type=jnp.float32)  13.9 us
    dot_general x4, matrix products, local_step(): share = jnp.dot(weight_rows, passages, preferred_element_type=jnp.float32)  11.6 us
  transfers between devices with their start and end apart: 24, of which 14 were waited for; matrix products, arithmetic and copies ran while one was open for 20% of the time, Pallas kernels for 0%

profile of v3, /device:TPU:0, one launch (start us, length us, event | category | flops | bytes accessed | tf_op | source)
XLA Modules:
  0.0 490.4 jit_solution(9048640698033327421)
XLA Ops:
  8.7 3.1 collective-permute-start.2
  11.7 2.6 collective-permute-start.1
  14.3 1.3 collective-permute-start
  19.8 3.0 convolution_convert_fusion
  22.9 3.7 all-to-all-start.3
  26.6 1.3 collective-permute-start.6
  27.9 4.6 collective-permute-start.3
  32.6 29.8 %collective-permute-done.6 = bf16[128,3584]{1,0:T(8,128)(2,1)S(1)} collective-permute-done((bf16[128,3584]{1,0:T(8,128)(2,1)S(1)}, bf16[128,3584]{1,0:T(8,128)(2,1)S(1)}, u32[]{:S(2)}, u32[]{:S(2)}) %collective-permute-start.6) | collective-permute-done | bytes 917536 | tf_op jit(solution)/shard_map/ppermute | solution.py:64
  64.3 1.9 convolution_convert_fusion.1
  66.2 4.3 all-to-all-start.2
  70.5 1.3 collective-permute-start.7
  72.6 42.4 %collective-permute-done.7 = bf16[128,3584]{1,0:T(8,128)(2,1)S(1)} collective-permute-done((bf16[128,3584]{1,0:T(8,128)(2,1)}, bf16[128,3584]{1,0:T(8,128)(2,1)S(1)}, u32[]{:S(2)}, u32[]{:S(2)}) %collective-permute-start.7) | collective-permute-done | bytes 917536 | tf_op jit(solution)/shard_map/ppermute | solution.py:64
  116.9 3.1 convolution_convert_fusion.2
  119.9 4.8 all-to-all-start.1
  124.7 1.3 collective-permute-start.8
  126.8 62.6 %collective-permute-done.8 = bf16[128,3584]{1,0:T(8,128)(2,1)S(1)} collective-permute-done((bf16[128,3584]{1,0:T(8,128)(2,1)}, bf16[128,3584]{1,0:T(8,128)(2,1)S(1)}, u32[]{:S(2)}, u32[]{:S(2)}) %collective-permute-start.8) | collective-permute-done | bytes 917536 | tf_op jit(solution)/shard_map/ppermute | solution.py:64
  189.4 1.9 convolution_convert_fusion.3
  191.3 4.3 all-to-all-start
  195.7 3.4 fusion.97
  199.4 3.4 fusion.98
  202.9 2.9 fusion.99
  206.9 3.7 fusion.100
  210.6 8.9 %all-to-all-done = bf16[8,32,3584]{2,1,0:T(8,128)(2,1)} async-done(((bf16[8,32,3584]{2,1,0:T(8,128)(2,1)}), bf16[8,32,3584]{2,1,0:T(8,128)(2,1)}, u32[]{:S(2)}, u32[]{:S(2)}) %all-to-all-start) | async-done | bytes 1835040 | tf_op jit(solution)/shard_map/all_to_all | solution.py:46
  219.5 3.9 fusion.101
  224.9 2.8 all-to-all-start.4
  228.0 6.9 %all-to-all-done.4 = f32[32,1,32]{2,1,0:T(1,128)S(1)} async-done(((f32[32,1,32]{2,1,0:T(1,128)}), f32[32,1,32]{2,1,0:T(1,128)S(1)}, u32[]{:S(2)}, u32[]{:S(2)}) %all-to-all-start.4) | async-done | bytes 4128 | tf_op jit(solution)/shard_map/all_to_all | solution.py:46
  238.1 2.7 all-to-all-start.5
  241.6 6.4 %all-to-all-done.5 = f32[32,1,32]{2,1,0:T(1,128)S(1)} async-done(((f32[32,1,32]{2,1,0:T(1,128)}), f32[32,1,32]{2,1,0:T(1,128)S(1)}, u32[]{:S(2)}, u32[]{:S(2)}) %all-to-all-start.5) | async-done | bytes 4128 | tf_op jit(solution)/shard_map/all_to_all | solution.py:46
  248.4 2.1 constant_dynamic-update-slice_fusion.3
  250.4 1.9 constant_dynamic-update-slice_fusion.2
  252.3 1.9 constant_dynamic-update-slice_fusion.1
  254.2 2.0 constant_dynamic-update-slice_fusion
  256.2 2.4 convolution_convert_fusion.5
  258.6 4.3 all-to-all-start.8
  263.0 4.4 convolution_convert_fusion.6
  267.5 19.3 %all-to-all-done.8 = bf16[8,32,3584]{2,1,0:T(8,128)(2,1)} async-done(((bf16[8,32,3584]{2,1,0:T(8,128)(2,1)}), bf16[8,32,3584]{2,1,0:T(8,128)(2,1)}, u32[]{:S(2)}, u32[]{:S(2)}) %all-to-all-start.8) | async-done | bytes 1835040 | tf_op jit(solution)/shard_map/all_to_all | solution.py:46
  286.7 4.3 all-to-all-start.7
  291.1 3.2 convolution_convert_fusion.11
  295.7 2.4 convolution_convert_fusion.7
  298.1 16.8 %all-to-all-done.7 = bf16[8,32,3584]{2,1,0:T(8,128)(2,1)} async-done(((bf16[8,32,3584]{2,1,0:T(8,128)(2,1)}), bf16[8,32,3584]{2,1,0:T(8,128)(2,1)}, u32[]{:S(2)}, u32[]{:S(2)}) %all-to-all-start.7) | async-done | bytes 1835040 | tf_op jit(solution)/shard_map/all_to_all | solution.py:46
  314.9 4.3 all-to-all-start.6
  319.2 1.4 constant_dynamic-update-slice_fusion.7
  320.6 3.1 constant_dynamic-update-slice_fusion.6
  323.7 2.8 constant_dynamic-update-slice_fusion.5
  326.5 2.4 convolution_convert_fusion.4
  328.9 14.1 %all-to-all-done.6 = bf16[8,32,3584]{2,1,0:T(8,128)(2,1)} async-done(((bf16[8,32,3584]{2,1,0:T(8,128)(2,1)}), bf16[8,32,3584]{2,1,0:T(8,128)(2,1)}, u32[]{:S(2)}, u32[]{:S(2)}) %all-to-all-start.6) | async-done | bytes 1835040 | tf_op jit(solution)/shard_map/all_to_all | solution.py:46
  343.0 3.6 all-to-all-start.9
  346.6 2.9 convolution_convert_fusion.8
  350.1 2.9 convolution_convert_fusion.10
  353.0 1.5 collective-permute-start.9
  354.5 2.9 convolution_convert_fusion.9
  358.4 2.8 constant_dynamic-update-slice_fusion.4
  361.3 1.9 fusion.5
  363.2 7.2 %all-to-all-done.9 = bf16[8,32,3584]{2,1,0:T(8,128)(2,1)S(1)} async-done(((bf16[8,32,3584]{2,1,0:T(8,128)(2,1)}), bf16[8,32,3584]{2,1,0:T(8,128)(2,1)S(1)}, u32[]{:S(2)}, u32[]{:S(2)}) %all-to-all-start.9) | async-done | bytes 1835040 | tf_op jit(solution)/shard_map/all_to_all | solution.py:46
  370.8 1.8 collective-permute-done.11
  372.6 58.9 %collective-permute-done.9 = bf16[128,3584]{1,0:T(8,128)(2,1)} collective-permute-done((bf16[128,3584]{1,0:T(8,128)(2,1)}, bf16[128,3584]{1,0:T(8,128)(2,1)}, u32[]{:S(2)}, u32[]{:S(2)}) %collective-permute-start.9) | collective-permute-done | bytes 917536 | tf_op jit(solution)/shard_map/ppermute | solution.py:237
  431.5 3.2 add_multiply_fusion
  434.8 19.9 %fusion.103 = f32[512,3584]{1,0:T(8,128)S(1)} fusion(bf16[512,3584]{1,0:T(8,128)(2,1)} %param.14, bf16[3584,3584]{1,0:T(8,128)(2,1)} %all-gather.2.cloned.1.call-done), kind=kOutput, calls=%fused_computation.239 | convolution fusion | flops 13153337344 | bytes 36700160 | tf_op jit(solution)/shard_map/dot_general | solution.py:88
  454.8 2.6 multiply_reduce_fusion
  457.4 2.5 fusion.3
  459.9 1.8 copy-done.7
  462.3 4.9 fusion.6
  468.4 3.9 all-to-all-start.10
  472.3 10.4 %convolution_multiply_fusion = f32[512,3584]{1,0:T(8,128)} fusion(bf16[1152,512]{1,0:T(8,128)(2,1)S(1)} %copy-done.26, bf16[1152,3584]{1,0:T(8,128)(2,1)} %constant_dynamic-update-slice_fusion.4), kind=kOutput, calls=%fused_computation.8 | convolution fusion | flops 4229693440 | bytes 16777216 | tf_op jit(solution)/shard_map/dot_general | solution.py:258
  (178 shorter events, 24.3 us)
Async XLA Ops:
  7.2 447.6 %copy-start = (bf16[16,3584]{1,0:T(8,128)(2,1)S(1)}, bf16[16,3584]{1,0:T(8,128)(2,1)}, u32[]{:S(2)}) copy-start(bf16[16,3584]{1,0:T(8,128)(2,1)} %param.18) | copy-start | bytes 344068
  7.2 427.6 %all-gather.2.cloned.1.call-start = ((), (), s32[]{:S(2)}) async-start(), calls=%async_computation.11 | async-start | bytes 26492928 | tf_op jit(solution)/shard_map/all_gather | solution.py:155
  8.7 7.8 %collective-permute-start.2 = (s32[32,4]{1,0:T(8,128)S(1)}, s32[32,4]{1,0:T(8,128)S(1)}, u32[]{:S(2)}, u32[]{:S(2)}) collective-permute-start(s32[32,4]{1,0:T(8,128)S(1)} %copy.38), channel_id=1, source_target_pairs={{0,8},{8,16},{16,24},{24,0},{1,9},{9,17},{17,25},{25,1},{2,10},{10... | collective-permute-start | bytes 1544 | tf_op jit(solution)/shard_map/ppermute | solution.py:160
  11.7 5.2 %collective-permute-start.1 = (s32[32,4]{1,0:T(8,128)S(1)}, s32[32,4]{1,0:T(8,128)S(1)}, u32[]{:S(2)}, u32[]{:S(2)}) collective-permute-start(s32[32,4]{1,0:T(8,128)S(1)} %copy.38), channel_id=1, source_target_pairs={{0,16},{8,24},{16,0},{24,8},{1,17},{9,25},{17,1},{25,9},{2,18},{10... | collective-permute-start | bytes 1544 | tf_op jit(solution)/shard_map/ppermute | solution.py:160
  14.3 3.7 collective-permute-start
  16.5 10.1 %copy-start.8 = (bf16[128,3584]{1,0:T(8,128)(2,1)S(1)}, bf16[128,3584]{1,0:T(8,128)(2,1)}, u32[]{:S(2)}) copy-start(bf16[128,3584]{1,0:T(8,128)(2,1)} %param.10) | copy-start | bytes 2752516
  22.9 43.3 %all-to-all-start.3 = ((bf16[8,32,3584]{2,1,0:T(8,128)(2,1)}), bf16[8,32,3584]{2,1,0:T(8,128)(2,1)S(1)}, u32[]{:S(2)}, u32[]{:S(2)}) async-start(bf16[8,32,3584]{2,1,0:T(8,128)(2,1)} %bitcast.98), calls=%async_computation.3 | async-start | bytes 3670016 | tf_op jit(solution)/shard_map/all_to_all | solution.py:46
  26.6 35.8 %collective-permute-start.6 = (bf16[128,3584]{1,0:T(8,128)(2,1)S(1)}, bf16[128,3584]{1,0:T(8,128)(2,1)S(1)}, u32[]{:S(2)}, u32[]{:S(2)}) collective-permute-start(bf16[128,3584]{1,0:T(8,128)(2,1)S(1)} %copy-done.8), channel_id=1, source_target_pairs={{8,0},{16,8},{24,16},{9,1},{17,9},{25,17},{10,2},{18,10},{26,18},{... | collective-permute-start | bytes 2752520 | tf_op jit(solution)/shard_map/ppermute | solution.py:64
  27.9 34.5 %collective-permute-start.3 = (bf16[128,3584]{1,0:T(8,128)(2,1)S(1)}, bf16[128,3584]{1,0:T(8,128)(2,1)S(1)}, u32[]{:S(2)}, u32[]{:S(2)}) collective-permute-start(bf16[128,3584]{1,0:T(8,128)(2,1)S(1)} %copy-done.8), channel_id=1, source_target_pairs={{0,8},{8,16},{16,24},{1,9},{9,17},{17,25},{2,10},{10,18},{18,26},{... | collective-permute-start | bytes 2752520 | tf_op jit(solution)/shard_map/ppermute | solution.py:63
  62.4 1.0 copy-start.25
  63.4 0.9 copy-start.36
  66.2 53.7 %all-to-all-start.2 = ((bf16[8,32,3584]{2,1,0:T(8,128)(2,1)}), bf16[8,32,3584]{2,1,0:T(8,128)(2,1)}, u32[]{:S(2)}, u32[]{:S(2)}) async-start(bf16[8,32,3584]{2,1,0:T(8,128)(2,1)} %bitcast.99), calls=%async_computation.2 | async-start | bytes 3670016 | tf_op jit(solution)/shard_map/all_to_all | solution.py:46
  70.5 44.5 %collective-permute-start.7 = (bf16[128,3584]{1,0:T(8,128)(2,1)}, bf16[128,3584]{1,0:T(8,128)(2,1)S(1)}, u32[]{:S(2)}, u32[]{:S(2)}) collective-permute-start(bf16[128,3584]{1,0:T(8,128)(2,1)} %copy-done.25), channel_id=1, source_target_pairs={{8,0},{16,8},{9,1},{17,9},{10,2},{18,10},{11,3},{19,11},{12,4},{20... | collective-permute-start | bytes 2752520 | tf_op jit(solution)/shard_map/ppermute | solution.py:64
  71.8 43.2 %collective-permute-start.4 = (bf16[128,3584]{1,0:T(8,128)(2,1)}, bf16[128,3584]{1,0:T(8,128)(2,1)S(1)}, u32[]{:S(2)}, u32[]{:S(2)}) collective-permute-start(bf16[128,3584]{1,0:T(8,128)(2,1)} %copy-done.36), channel_id=1, source_target_pairs={{8,16},{16,24},{9,17},{17,25},{10,18},{18,26},{11,19},{19,27},{12,... | collective-permute-start | bytes 2752520 | tf_op jit(solution)/shard_map/ppermute | solution.py:63
  115.0 0.9 copy-start.15
  115.9 0.9 copy-start.16
  119.9 71.4 %all-to-all-start.1 = ((bf16[8,32,3584]{2,1,0:T(8,128)(2,1)}), bf16[8,32,3584]{2,1,0:T(8,128)(2,1)}, u32[]{:S(2)}, u32[]{:S(2)}) async-start(bf16[8,32,3584]{2,1,0:T(8,128)(2,1)} %bitcast.96), calls=%async_computation.1 | async-start | bytes 3670016 | tf_op jit(solution)/shard_map/all_to_all | solution.py:46
  124.7 64.7 %collective-permute-start.8 = (bf16[128,3584]{1,0:T(8,128)(2,1)}, bf16[128,3584]{1,0:T(8,128)(2,1)S(1)}, u32[]{:S(2)}, u32[]{:S(2)}) collective-permute-start(bf16[128,3584]{1,0:T(8,128)(2,1)} %copy-done.15), channel_id=1, source_target_pairs={{8,0},{9,1},{10,2},{11,3},{12,4},{13,5},{14,6},{15,7}} | collective-permute-start | bytes 2752520 | tf_op jit(solution)/shard_map/ppermute | solution.py:64
  126.0 63.4 %collective-permute-start.5 = (bf16[128,3584]{1,0:T(8,128)(2,1)}, bf16[128,3584]{1,0:T(8,128)(2,1)S(1)}, u32[]{:S(2)}, u32[]{:S(2)}) collective-permute-start(bf16[128,3584]{1,0:T(8,128)(2,1)} %copy-done.16), channel_id=1, source_target_pairs={{16,24},{17,25},{18,26},{19,27},{20,28},{21,29},{22,30},{23,31}} | collective-permute-start | bytes 2752520 | tf_op jit(solution)/shard_map/ppermute | solution.py:63
  191.3 28.1 %all-to-all-start = ((bf16[8,32,3584]{2,1,0:T(8,128)(2,1)}), bf16[8,32,3584]{2,1,0:T(8,128)(2,1)}, u32[]{:S(2)}, u32[]{:S(2)}) async-start(bf16[8,32,3584]{2,1,0:T(8,128)(2,1)} %bitcast.92), calls=%async_computation | async-start | bytes 3670016 | tf_op jit(solution)/shard_map/all_to_all | solution.py:46
  199.1 37.5 %copy-start.27 = (f32[128]{0:T(128)}, f32[128]{0:T(128)S(1)}, u32[]{:S(2)}) copy-start(f32[128]{0:T(128)S(1)} %get-tuple-element.43) | copy-start | bytes 1540
  199.1 41.7 %copy-start.18 = (f32[128,512]{1,0:T(8,128)}, f32[128,512]{1,0:T(8,128)S(1)}, u32[]{:S(2)}) copy-start(f32[128,512]{1,0:T(8,128)S(1)} %get-tuple-element.44) | copy-start | bytes 786436
  199.2 3.6 copy-start.1
  199.4 37.2 %copy-start.31 = (f32[128]{0:T(128)}, f32[128]{0:T(128)S(1)}, u32[]{:S(2)}) copy-start(f32[128]{0:T(128)S(1)} %fusion.57) | copy-start | bytes 1540
  202.8 4.0 copy-start.23
  205.8 0.8 copy-start.21
  219.5 3.9 copy-start.22
  219.5 21.3 %copy-start.33 = (s32[128]{0:T(128)S(1)}, s32[128]{0:T(128)}, u32[]{:S(2)}) copy-start(s32[128]{0:T(128)} %param.13) | copy-start | bytes 1540
  223.4 0.8 copy-start.24
  224.9 10.0 %all-to-all-start.4 = ((f32[32,1,32]{2,1,0:T(1,128)}), f32[32,1,32]{2,1,0:T(1,128)S(1)}, u32[]{:S(2)}, u32[]{:S(2)}) async-start(f32[32,1,32]{2,1,0:T(1,128)} %all_to_all.41), calls=%async_computation.4 | async-start | bytes 32768 | tf_op jit(solution)/shard_map/all_to_all | solution.py:46
  238.1 9.9 %all-to-all-start.5 = ((f32[32,1,32]{2,1,0:T(1,128)}), f32[32,1,32]{2,1,0:T(1,128)S(1)}, u32[]{:S(2)}, u32[]{:S(2)}) async-start(f32[32,1,32]{2,1,0:T(1,128)} %select_n.957), calls=%async_computation.5 | async-start | bytes 32768 | tf_op jit(solution)/shard_map/all_to_all | solution.py:46
  248.4 7.8 %copy-start.2 = (bf16[512,3584]{1,0:T(8,128)(2,1)S(1)}, bf16[512,3584]{1,0:T(8,128)(2,1)}, u32[]{:S(2)}) copy-start(bf16[512,3584]{1,0:T(8,128)(2,1)} %param.11) | copy-start | bytes 11010052
  254.2 4.4 copy-start.9
  256.2 2.4 copy-start.12
  256.2 6.8 %copy-start.29 = (bf16[3584]{0:T(1024)(128)(2,1)S(1)}, bf16[3584]{0:T(1024)(128)(2,1)}, u32[]{:S(2)}) copy-start(bf16[3584]{0:T(1024)(128)(2,1)} %param.19) | copy-start | bytes 21508
  258.6 28.1 %all-to-all-start.8 = ((bf16[8,32,3584]{2,1,0:T(8,128)(2,1)}), bf16[8,32,3584]{2,1,0:T(8,128)(2,1)}, u32[]{:S(2)}, u32[]{:S(2)}) async-start(bf16[8,32,3584]{2,1,0:T(8,128)(2,1)} %bitcast.93), calls=%async_computation.8 | async-start | bytes 3670016 | tf_op jit(solution)/shard_map/all_to_all | solution.py:46
  286.7 28.1 %all-to-all-start.7 = ((bf16[8,32,3584]{2,1,0:T(8,128)(2,1)}), bf16[8,32,3584]{2,1,0:T(8,128)(2,1)}, u32[]{:S(2)}, u32[]{:S(2)}) async-start(bf16[8,32,3584]{2,1,0:T(8,128)(2,1)} %bitcast.95), calls=%async_computation.7 | async-start | bytes 3670016 | tf_op jit(solution)/shard_map/all_to_all | solution.py:46
  291.1 4.5 copy-start.30
  291.1 4.6 copy-start.3
  291.1 4.6 copy-start.10
  291.1 4.6 copy-start.13
  314.9 28.1 %all-to-all-start.6 = ((bf16[8,32,3584]{2,1,0:T(8,128)(2,1)}), bf16[8,32,3584]{2,1,0:T(8,128)(2,1)}, u32[]{:S(2)}, u32[]{:S(2)}) async-start(bf16[8,32,3584]{2,1,0:T(8,128)(2,1)} %bitcast.97), calls=%async_computation.6 | async-start | bytes 3670016 | tf_op jit(solution)/shard_map/all_to_all | solution.py:46
  320.6 6.0 %copy-start.4 = (bf16[512,3584]{1,0:T(8,128)(2,1)S(1)}, bf16[512,3584]{1,0:T(8,128)(2,1)}, u32[]{:S(2)}) copy-start(bf16[512,3584]{1,0:T(8,128)(2,1)} %param.11) | copy-start | bytes 11010052
  320.6 6.0 %copy-start.11 = (bf16[256,512]{1,0:T(8,128)(2,1)S(1)}, bf16[256,512]{1,0:T(8,128)(2,1)}, u32[]{:S(2)}) copy-start(bf16[256,512]{1,0:T(8,128)(2,1)} %copy-done.9) | copy-start | bytes 786436
  320.6 6.0 %copy-start.14 = (bf16[256,512]{1,0:T(8,128)(2,1)S(1)}, bf16[256,512]{1,0:T(8,128)(2,1)}, u32[]{:S(2)}) copy-start(bf16[256,512]{1,0:T(8,128)(2,1)} %copy-done.12) | copy-start | bytes 786436
  343.0 27.3 %all-to-all-start.9 = ((bf16[8,32,3584]{2,1,0:T(8,128)(2,1)}), bf16[8,32,3584]{2,1,0:T(8,128)(2,1)S(1)}, u32[]{:S(2)}, u32[]{:S(2)}) async-start(bf16[8,32,3584]{2,1,0:T(8,128)(2,1)} %bitcast.94), calls=%async_computation.9 | async-start | bytes 3670016 | tf_op jit(solution)/shard_map/all_to_all | solution.py:46
  349.5 23.1 %collective-permute-start.11 = (bf16[128,3584]{1,0:T(8,128)(2,1)}, bf16[128,3584]{1,0:T(8,128)(2,1)S(1)}, u32[]{:S(2)}, u32[]{:S(2)}) collective-permute-start(bf16[128,3584]{1,0:T(8,128)(2,1)} %convolution_convert_fusion.8), channel_id=1, source_target_pairs={{0,24},{8,0},{16,8},{24,16},{1,25},{9,1},{17,9},{25,17},{2,26},{10... | collective-permute-start | bytes 2752520 | tf_op jit(solution)/shard_map/ppermute | solution.py:237
  353.0 8.2 %copy-start.5 = (bf16[512,3584]{1,0:T(8,128)(2,1)S(1)}, bf16[512,3584]{1,0:T(8,128)(2,1)}, u32[]{:S(2)}) copy-start(bf16[512,3584]{1,0:T(8,128)(2,1)} %param.11) | copy-start | bytes 11010052
  353.0 8.2 %copy-start.19 = (f32[128,512]{1,0:T(8,128)S(1)}, f32[128,512]{1,0:T(8,128)}, u32[]{:S(2)}) copy-start(f32[128,512]{1,0:T(8,128)} %copy-done.18) | copy-start | bytes 786436
  353.0 8.2 %copy-start.28 = (f32[128]{0:T(128)S(1)}, f32[128]{0:T(128)}, u32[]{:S(2)}) copy-start(f32[128]{0:T(128)} %copy-done.27) | copy-start | bytes 1540
  353.0 8.2 %copy-start.32 = (f32[128]{0:T(128)S(1)}, f32[128]{0:T(128)}, u32[]{:S(2)}) copy-start(f32[128]{0:T(128)} %copy-done.31) | copy-start | bytes 1540
  353.0 8.2 %copy-start.35 = (f32[128]{0:T(128)S(1)}, f32[128]{0:T(128)}, u32[]{:S(2)}) copy-start(f32[128]{0:T(128)} %get-tuple-element.20) | copy-start | bytes 1540
  353.0 78.5 %collective-permute-start.9 = (bf16[128,3584]{1,0:T(8,128)(2,1)}, bf16[128,3584]{1,0:T(8,128)(2,1)}, u32[]{:S(2)}, u32[]{:S(2)}) collective-permute-start(bf16[128,3584]{1,0:T(8,128)(2,1)} %convolution_convert_fusion.10), channel_id=1, source_target_pairs={{0,16},{8,24},{16,0},{24,8},{1,17},{9,25},{17,1},{25,9},{2,18},{10... | collective-permute-start | bytes 2752520 | tf_op jit(solution)/shard_map/ppermute | solution.py:237
  357.5 74.0 %collective-permute-start.10 = (bf16[128,3584]{1,0:T(8,128)(2,1)}, bf16[128,3584]{1,0:T(8,128)(2,1)}, u32[]{:S(2)}, u32[]{:S(2)}) collective-permute-start(bf16[128,3584]{1,0:T(8,128)(2,1)} %convolution_convert_fusion.9), channel_id=1, source_target_pairs={{0,8},{8,16},{16,24},{24,0},{1,9},{9,17},{17,25},{25,1},{2,10},{10... | collective-permute-start | bytes 2752520 | tf_op jit(solution)/shard_map/ppermute | solution.py:237
  363.2 68.3 %copy-start.34 = (s32[128]{0:T(128)S(1)}, s32[128]{0:T(128)}, u32[]{:S(2)}) copy-start(s32[128]{0:T(128)} %param.13) | copy-start | bytes 1540
  370.4 61.1 %copy-start.6 = (bf16[512,3584]{1,0:T(8,128)(2,1)S(1)}, bf16[512,3584]{1,0:T(8,128)(2,1)}, u32[]{:S(2)}) copy-start(bf16[512,3584]{1,0:T(8,128)(2,1)} %param.11) | copy-start | bytes 11010052
  434.7 20.0 %copy-start.20 = (f32[128,3584]{1,0:T(8,128)}, f32[128,3584]{1,0:T(8,128)S(1)}, u32[]{:S(2)}) copy-start(f32[128,3584]{1,0:T(8,128)S(1)} %add_multiply_fusion) | copy-start | bytes 5505028
  434.8 20.0 %copy-start.17 = (bf16[512,3584]{1,0:T(8,128)(2,1)S(1)}, bf16[512,3584]{1,0:T(8,128)(2,1)}, u32[]{:S(2)}) copy-start(bf16[512,3584]{1,0:T(8,128)(2,1)} %param.15) | copy-start | bytes 11010052
  459.9 1.8 copy-start.7
  462.3 9.9 %copy-start.26 = (bf16[1152,512]{1,0:T(8,128)(2,1)S(1)}, bf16[1152,512]{1,0:T(8,128)(2,1)}, u32[]{:S(2)}) copy-start(bf16[1152,512]{1,0:T(8,128)(2,1)} %get-tuple-element.12) | copy-start | bytes 3538948
  468.4 14.5 %all-to-all-start.10 = ((bf16[32,32,112]{2,1,0:T(8,128)(2,1)}), bf16[32,32,112]{2,1,0:T(8,128)(2,1)S(1)}, u32[]{:S(2)}, u32[]{:S(2)}) async-start(bf16[32,32,112]{2,1,0:T(8,128)(2,1)} %bitcast.88), calls=%async_computation.10 | async-start | bytes 524288 | tf_op jit(solution)/shard_map/all_to_all | solution.py:46
Sparse Core Ops, SparseCore 0:
  10.8 208.2 all-gather.1
